TPU v7x, 32 devices: a whole 2x2x4 slice. The times are simulated.
32 devices in a mesh: fsdp: 32 (over z, y, x, core).
Axes of the slice: x: 2, y: 2, z: 4, core: 2. Of those that a mesh axis runs over, the one named last changes fastest.
Arguments:
- tok_ids: int32 [32768], P('fsdp')
- tok_labels: int32 [32768], P('fsdp')
- loss_mask: int32 [32768], P('fsdp')
- emb_table: bfloat16 [20480, 256], P('fsdp')
- gain_mlp: float32 [256], replicated
- gain_head: float32 [256], replicated
- w_gate: bfloat16 [256, 2048], P('fsdp')
- w_up: bfloat16 [256, 2048], P('fsdp')
- w_down: bfloat16 [2048, 256], P('fsdp')
Outputs:
- output 1: float32 [], replicated
- output 2: float32 [20480, 256], P('fsdp')
- output 3: float32 [256, 2048], P('fsdp')
- output 4: float32 [256, 2048], P('fsdp')
- output 5: float32 [2048, 256], P('fsdp')
All inputs are finite; a program needn't handle non-finite values.
Results may differ from a plain program's by a relative error of at most 0.00898581.
Values are sent between devices in bfloat16 or wider.
A program may use at most 1 GiB of HBM per device.

v0:
```python
import jax
import jax.numpy as jnp
from jax import lax
from jax.sharding import PartitionSpec as P

NORM_EPS = 1e-6
ROW_CONTRACT = (((1,), (1,)), ((), ()))
TOK_CONTRACT = (((0,), (0,)), ((), ()))


def rms_scale(rows_wide, norm_gain):
    inv_rms = lax.rsqrt(jnp.mean(rows_wide * rows_wide, axis=-1, keepdims=True) + NORM_EPS)
    return (rows_wide * inv_rms * norm_gain).astype(jnp.bfloat16), inv_rms


def rms_back(rows_wide, inv_rms, norm_gain, grad_out):
    scaled_grad = grad_out * norm_gain
    return inv_rms * (scaled_grad - rows_wide * (inv_rms * inv_rms) * jnp.mean(scaled_grad * rows_wide, axis=-1, keepdims=True))


def mlp_forward(emb_rows, gain_mlp, gain_head, w_gate, w_up, w_down):
    emb_wide = emb_rows.astype(jnp.float32)
    a_norm, inv_first = rms_scale(emb_wide, gain_mlp)
    gate_wide = jnp.dot(a_norm, w_gate, preferred_element_type=jnp.float32).astype(jnp.bfloat16).astype(jnp.float32)
    up_wide = jnp.dot(a_norm, w_up, preferred_element_type=jnp.float32).astype(jnp.bfloat16).astype(jnp.float32)
    gate_sig = jax.nn.sigmoid(gate_wide)
    act_rows = (gate_wide * gate_sig * up_wide).astype(jnp.bfloat16)
    hid_wide = (emb_wide + jnp.dot(act_rows, w_down, preferred_element_type=jnp.float32)).astype(jnp.bfloat16).astype(jnp.float32)
    h_norm, inv_second = rms_scale(hid_wide, gain_head)
    return (emb_wide, inv_first, a_norm, gate_wide, up_wide, gate_sig, act_rows, hid_wide, inv_second), h_norm


def head_forward(h_norm, emb_table, tok_labels, tok_coef):
    logits = lax.dot_general(h_norm, emb_table, ROW_CONTRACT, preferred_element_type=jnp.float32)
    row_max = jnp.max(logits, axis=-1, keepdims=True)
    exp_rows = jnp.exp(logits - row_max)
    sum_exp = jnp.sum(exp_rows, axis=-1, keepdims=True)
    is_label = jnp.arange(logits.shape[1])[None, :] == tok_labels[:, None]
    picked = jnp.sum(jnp.where(is_label, logits, 0.0), axis=-1)
    tok_loss = row_max[:, 0] + jnp.log(sum_exp[:, 0]) - picked
    d_logits = ((exp_rows / sum_exp - is_label.astype(jnp.float32)) * tok_coef[:, None]).astype(jnp.bfloat16)
    return jnp.sum(tok_coef * tok_loss), d_logits


def mlp_backward(saved, d_hidden, gain_mlp, w_gate, w_up, w_down):
    emb_wide, inv_first, a_norm, gate_wide, up_wide, gate_sig, act_rows = saved[:7]
    hid_grad = d_hidden.astype(jnp.bfloat16)
    d_act = lax.dot_general(hid_grad, w_down, ROW_CONTRACT, preferred_element_type=jnp.float32)
    grad_down = lax.dot_general(act_rows, hid_grad, TOK_CONTRACT, preferred_element_type=jnp.float32)
    d_up = (d_act * gate_wide * gate_sig).astype(jnp.bfloat16)
    d_gate = (d_act * up_wide * gate_sig * (1.0 + gate_wide * (1.0 - gate_sig))).astype(jnp.bfloat16)
    grad_gate = lax.dot_general(a_norm, d_gate, TOK_CONTRACT, preferred_element_type=jnp.float32)
    grad_up = lax.dot_general(a_norm, d_up, TOK_CONTRACT, preferred_element_type=jnp.float32)
    d_anorm = lax.dot_general(d_gate, w_gate, ROW_CONTRACT, preferred_element_type=jnp.float32) + lax.dot_general(d_up, w_up, ROW_CONTRACT, preferred_element_type=jnp.float32)
    grad_x = d_hidden + rms_back(emb_wide, inv_first, gain_mlp, d_anorm)
    return grad_x, grad_gate, grad_up, grad_down


def solution(mesh):
    def gather_rows(row_shard):
        return lax.all_gather(row_shard, "fsdp", axis=0, tiled=True)

    def scatter_rows(full_rows):
        return lax.psum_scatter(full_rows, "fsdp", scatter_dimension=0, tiled=True)

    def device_step(tok_ids, tok_labels, loss_mask, table_shard, gain_mlp, gain_head, gate_shard, up_shard, down_shard):
        mask_wide = loss_mask.astype(jnp.float32)
        tok_coef = mask_wide / lax.psum(jnp.sum(mask_wide), "fsdp")
        table_full = gather_rows(table_shard)
        gate_full = gather_rows(gate_shard)
        up_full = gather_rows(up_shard)
        down_full = gather_rows(down_shard)
        emb_rows = jnp.take(table_full, tok_ids, axis=0)
        saved, h_norm = mlp_forward(emb_rows, gain_mlp, gain_head, gate_full, up_full, down_full)
        loss_part, d_logits = head_forward(h_norm, table_full, tok_labels, tok_coef)
        table_again, d_logits = lax.optimization_barrier((table_shard, d_logits))
        table_back = gather_rows(table_again)
        d_hnorm = jnp.dot(d_logits, table_back, preferred_element_type=jnp.float32)
        head_grad = lax.dot_general(d_logits, h_norm, TOK_CONTRACT, preferred_element_type=jnp.float32)
        d_hidden = rms_back(saved[7], saved[8], gain_head, d_hnorm)
        gate_again, up_again, down_again, d_hidden = lax.optimization_barrier((gate_shard, up_shard, down_shard, d_hidden))
        gate_back = gather_rows(gate_again)
        up_back = gather_rows(up_again)
        down_back = gather_rows(down_again)
        grad_x, grad_gate, grad_up, grad_down = mlp_backward(saved, d_hidden, gain_mlp, gate_back, up_back, down_back)
        grad_table = head_grad + jax.ops.segment_sum(grad_x, tok_ids, num_segments=table_back.shape[0])
        return (lax.psum(loss_part, "fsdp"), scatter_rows(grad_table), scatter_rows(grad_gate), scatter_rows(grad_up), scatter_rows(grad_down))

    row_spec = P("fsdp", None)
    tok_spec = P("fsdp")
    return jax.shard_map(device_step, mesh=mesh, in_specs=(tok_spec, tok_spec, tok_spec, row_spec, P(), P(), row_spec, row_spec, row_spec), out_specs=(P(), row_spec, row_spec, row_spec, row_spec), check_vma=False)
```

profile of v0, /device:TPU:0, one launch (start us, length us, event | category | flops | bytes accessed | tf_op | source)
XLA Modules:
  0.0 1290.5 jit_solution(1500407775033608198)
XLA Ops:
  7.2 0.0 all-gather.9.cloned.1.call-start
  7.2 0.7 all-gather.9.cloned.1.call-update
  7.9 0.0 all-gather.11.cloned.1.call-start
  8.0 0.7 all-gather.11.cloned.1.call-update
  8.7 0.0 all-gather.13.cloned.1.call-start
  8.7 0.7 all-gather.13.cloned.1.call-update
  9.4 0.0 all-gather.15.cloned.1.call-start
  9.4 0.5 all-gather.15.cloned.1.call-update
  10.0 0.0 all-gather.17.cloned.1.call-start
  10.0 1.3 convert_reduce_fusion
  11.3 0.7 fusion.36
  12.0 0.7 compare_and_fusion
  12.7 42.8 %psum.14 = f32[]{:T(128)} all-reduce(f32[]{:T(128)} %convert_reduce_fusion), channel_id=1, replica_groups=mesh['fsdp'=32] {'fsdp'}, use_global_device_ids=true, to_apply=%region_1.0 | all-reduce | flops 1 | bytes 8 | tf_op jit(solution)/shard_map/psum | solution.py:68
  55.5 44.3 %all-gather.9.cloned.1.call-done = bf16[20480,256]{1,0:T(8,128)(2,1)} async-done(((bf16[640,256]{1,0:T(8,128)(2,1)}), bf16[20480,256]{1,0:T(8,128)(2,1)}) %all-gather.9.cloned.1.call-update) | async-done | bytes 10485776 | tf_op jit(solution)/shard_map/all_gather | solution.py:61
  99.8 8.8 gather_fusion
  108.6 0.2 copy.15
  108.8 0.2 fusion.20
  108.9 0.6 fusion.37
  109.5 45.5 %all-gather.11.cloned.1.call-done = bf16[256,2048]{1,0:T(8,128)(2,1)} async-done(((bf16[8,2048]{1,0:T(8,128)(2,1)}), bf16[256,2048]{1,0:T(8,128)(2,1)}) %all-gather.11.cloned.1.call-update) | async-done | bytes 1048592 | tf_op jit(solution)/shard_map/all_gather | solution.py:61
  155.0 4.5 convolution_convert_fusion.1
  159.6 50.8 %all-gather.13.cloned.1.call-done = bf16[256,2048]{1,0:T(8,128)(2,1)} async-done(((bf16[8,2048]{1,0:T(8,128)(2,1)}), bf16[256,2048]{1,0:T(8,128)(2,1)}) %all-gather.13.cloned.1.call-update) | async-done | bytes 1048592 | tf_op jit(solution)/shard_map/all_gather | solution.py:61
  210.4 6.9 fusion.1
  217.3 48.3 %all-gather.15.cloned.1.call-done = bf16[2048,256]{1,0:T(8,128)(2,1)} async-done(((bf16[64,256]{1,0:T(8,128)(2,1)}), bf16[2048,256]{1,0:T(8,128)(2,1)}) %all-gather.15.cloned.1.call-update) | async-done | bytes 1048592 | tf_op jit(solution)/shard_map/all_gather | solution.py:61
  265.6 3.8 fusion.13
  269.5 36.6 %fusion.45 = (f32[1024]{0:T(1024)S(1)}, f32[1024,20480]{1,0:T(8,128)}) fusion(bf16[20480,256]{1,0:T(8,128)(2,1)} %all-gather.9.cloned.1.call-done, bf16[1024,256]{0,1:T(8,128)(2,1)S(1)} %get-tuple-element.30, f32[256]{0:T(256)S(1)} %copy-done, f32[1024]{0:T(1024)S(1)} %get-tuple-element.26), kind=kOutput, calls=%fused_computation.74 | convolution fusion | flops 10759437312 | bytes 94905344 | tf_op jit(solution)/shard_map/dot_general | solution.py:34
  306.1 27.3 %fusion = (f32[1024]{0:T(1024)S(1)}, f32[1024]{0:T(1024)S(1)}) fusion(f32[1024,20480]{1,0:T(8,128)} %get-tuple-element.32, f32[1024]{0:T(1024)S(1)} %get-tuple-element.31, s32[1024]{0:T(1024)S(1)} %copy-done.2), kind=kLoop, calls=%fused_computation.6 | loop fusion | flops 104855552 | bytes 83902464 | tf_op jit(solution)/shard_map/reduce_sum | solution.py:37
  333.4 1.3 multiply_reduce_fusion
  334.7 42.4 %multiply_convert_fusion = bf16[1024,20480]{1,0:T(8,128)(2,1)} fusion(f32[1024,20480]{1,0:T(8,128)} %get-tuple-element.32, f32[1024]{0:T(1024)S(1)} %get-tuple-element.20, f32[1024]{0:T(1024)S(1)} %get-tuple-element.17, s32[1024]{0:T(1024)S(1)} %copy-done.2, f32[1024]{0:T(1024)S(1)} %get-tuple-element.31), kind=kLoop, calls=%fused_computation.2 | loop fusion | flops 146800640 | bytes 125845504 | tf_op jit(solution)/shard_map/convert_element_type | solution.py:41
  377.1 0.0 all-gather.17.cloned.1.call-update
  377.1 0.0 all-gather.19.cloned.1.call-start
  377.2 85.0 %all-gather.17.cloned.1.call-done = bf16[20480,256]{1,0:T(8,128)(2,1)} async-done(((bf16[640,256]{1,0:T(8,128)(2,1)}), bf16[20480,256]{1,0:T(8,128)(2,1)}) %all-gather.17.cloned.1.call-update) | async-done | bytes 10485776 | tf_op jit(solution)/shard_map/all_gather | solution.py:61
  462.2 19.8 %fusion.19 = (f32[1024]{0:T(1024)S(1)}, f32[1024,256]{0,1:T(8,128)S(1)}) fusion(bf16[1024,256]{0,1:T(8,128)(2,1)S(1)} %get-tuple-element.30, f32[256]{0:T(256)S(1)} %copy-done, bf16[1024,20480]{1,0:T(8,128)(2,1)} %multiply_convert_fusion, bf16[20480,256]{1,0:T(8,128)(2,1)} %all-gather.17.cloned.1.call-done), kind=kOutput, calls=%fused_computation.44 | convolution fusion | flops 10738465792 | bytes 54006784 | tf_op jit(solution)/shard_map/dot_general | solution.py:78
  482.0 0.2 fusion.18
  482.2 0.0 all-gather.19.cloned.1.call-update
  482.2 0.0 all-gather.21.cloned.1.call-start
  482.3 0.7 all-gather.21.cloned.1.call-update
  483.0 0.0 all-gather.23.cloned.1.call-start
  483.0 0.7 all-gather.23.cloned.1.call-update
  483.7 0.0 reduce-scatter.11.cloned.1.call-start
  483.8 4.9 fusion.28
  488.7 0.0 reduce-scatter.11.cloned.1.call-update
  488.7 0.0 reduce-scatter.7.cloned.1.call-start
  488.7 46.0 %all-gather.19.cloned.1.call-done = bf16[2048,256]{1,0:T(8,128)(2,1)} async-done(((bf16[64,256]{1,0:T(8,128)(2,1)}), bf16[2048,256]{1,0:T(8,128)(2,1)}) %all-gather.19.cloned.1.call-update) | async-done | bytes 1048592 | tf_op jit(solution)/shard_map/all_gather | solution.py:61
  534.8 8.5 fusion.10
  543.2 2.0 copy-done.6
  545.2 2.7 fusion.41
  547.9 0.0 reduce-scatter.7.cloned.1.call-update
  547.9 0.0 reduce-scatter.9.cloned.1.call-start
  548.0 4.8 fusion.39
  552.8 0.0 reduce-scatter.5.cloned.1.call-start
  552.9 26.0 %fusion.32 = f32[20480,256]{1,0:T(8,128)} fusion(bf16[1024,20480]{1,0:T(8,128)(2,1)} %multiply_convert_fusion, bf16[1024,256]{0,1:T(8,128)(2,1)S(1)} %get-tuple-element.30, f32[256]{0:T(256)S(1)} %copy-done, f32[1024]{0:T(1024)S(1)} %get-tuple-element.26), kind=kOutput, calls=%fused_computation.58 | convolution fusion | flops 10738466816 | bytes 63443968 | tf_op jit(solution)/shard_map/dot_general | solution.py:79
  578.9 11.2 all-gather.21.cloned.1.call-done
  590.1 3.8 fusion.46
  593.9 51.6 %all-gather.23.cloned.1.call-done = bf16[256,2048]{1,0:T(8,128)(2,1)} async-done(((bf16[8,2048]{1,0:T(8,128)(2,1)}), bf16[256,2048]{1,0:T(8,128)(2,1)}) %all-gather.23.cloned.1.call-update) | async-done | bytes 1048592 | tf_op jit(solution)/shard_map/all_gather | solution.py:61
  645.5 3.8 fusion.27
  649.3 0.3 fusion.26
  649.6 0.3 copy.16
  650.0 19.9 %scatter_fusion = f32[20480,256]{1,0:T(8,128)} fusion(f32[20480,256]{1,0:T(8,128)} %fusion.32, s32[1024]{0:T(1024)S(1)} %copy-done.1, f32[1024,256]{1,0:T(8,128)S(1)} %copy.16), kind=kCustom, calls=%fused_computation.1 | custom fusion | flops 262144 | bytes 3149824 | tf_op jit(solution)/shard_map/scatter-add | solution.py:86
  669.9 0.0 reduce-scatter.5.cloned.1.call-update
  669.9 39.8 %psum.15 = f32[]{:T(128)} all-reduce(f32[]{:T(128)} %get-tuple-element.19), channel_id=1, replica_groups=mesh['fsdp'=32] {'fsdp'}, use_global_device_ids=true, to_apply=%region_8.9 | all-reduce | flops 1 | bytes 8 | tf_op jit(solution)/shard_map/psum | solution.py:87
  709.7 76.0 %reduce-scatter.11.cloned.1.call-done = f32[64,256]{1,0:T(8,128)} async-done(((f32[2048,256]{1,0:T(8,128)}), f32[64,256]{1,0:T(8,128)}) %reduce-scatter.11.cloned.1.call-update) | async-done | bytes 65552 | tf_op jit(solution)/shard_map/reduce_scatter | solution.py:64
  785.7 137.0 %reduce-scatter.7.cloned.1.call-done = f32[8,2048]{1,0:T(8,128)} async-done(((f32[256,2048]{1,0:T(8,128)}), f32[8,2048]{1,0:T(8,128)}) %reduce-scatter.7.cloned.1.call-update) | async-done | bytes 65552 | tf_op jit(solution)/shard_map/reduce_scatter | solution.py:64
  922.7 137.1 %reduce-scatter.9.cloned.1.call-done = f32[8,2048]{1,0:T(8,128)} async-done(((f32[256,2048]{1,0:T(8,128)}), f32[8,2048]{1,0:T(8,128)}) %reduce-scatter.9.cloned.1.call-update) | async-done | bytes 65552 | tf_op jit(solution)/shard_map/reduce_scatter | solution.py:64
  1059.9 223.8 %reduce-scatter.5.cloned.1.call-done = f32[640,256]{1,0:T(8,128)} async-done(((f32[20480,256]{1,0:T(8,128)}), f32[640,256]{1,0:T(8,128)}) %reduce-scatter.5.cloned.1.call-update) | async-done | bytes 655376 | tf_op jit(solution)/shard_map/reduce_scatter | solution.py:64
  (17 shorter events, 0.1 us)
Async XLA Ops:
  7.2 203.2 %copy-start.5 = (f32[256]{0:T(256)S(1)}, f32[256]{0:T(256)}, u32[]{:S(2)}) copy-start(f32[256]{0:T(256)} %param.13) | copy-start | bytes 3076
  7.2 92.6 %all-gather.9.cloned.1.call-start = ((), (), s32[]{:S(2)}) async-start(), calls=%async_computation.4 | async-start | bytes 10813440 | tf_op jit(solution)/shard_map/all_gather | solution.py:61
  7.9 147.1 %all-gather.11.cloned.1.call-start = ((), (), s32[]{:S(2)}) async-start(), calls=%async_computation.5 | async-start | bytes 1081344 | tf_op jit(solution)/shard_map/all_gather | solution.py:61
  8.7 201.7 %all-gather.13.cloned.1.call-start = ((), (), s32[]{:S(2)}) async-start(), calls=%async_computation.6 | async-start | bytes 1081344 | tf_op jit(solution)/shard_map/all_gather | solution.py:61
  9.4 256.2 %all-gather.15.cloned.1.call-start = ((), (), s32[]{:S(2)}) async-start(), calls=%async_computation.7 | async-start | bytes 1081344 | tf_op jit(solution)/shard_map/all_gather | solution.py:61
  10.0 452.2 %all-gather.17.cloned.1.call-start = ((), (), s32[]{:S(2)}) async-start(), calls=%async_computation.8 | async-start | bytes 10813440 | tf_op jit(solution)/shard_map/all_gather | solution.py:61
  217.3 52.2 %copy-start = (f32[256]{0:T(256)S(1)}, f32[256]{0:T(256)}, u32[]{:S(2)}) copy-start(f32[256]{0:T(256)} %param.14) | copy-start | bytes 3076
  269.4 36.6 %copy-start.2 = (s32[1024]{0:T(1024)S(1)}, s32[1024]{0:T(1024)}, u32[]{:S(2)}) copy-start(s32[1024]{0:T(1024)} %param.10) | copy-start | bytes 12292
  306.1 27.3 %copy-start.4 = (s32[1024]{0:T(1024)S(1)}, s32[1024]{0:T(1024)}, u32[]{:S(2)}) copy-start(s32[1024]{0:T(1024)} %param.11) | copy-start | bytes 12292
  377.1 157.6 %all-gather.19.cloned.1.call-start = ((), (), s32[]{:S(2)}) async-start(), calls=%async_computation.9 | async-start | bytes 1081344 | tf_op jit(solution)/shard_map/all_gather | solution.py:61
  482.2 107.9 %all-gather.21.cloned.1.call-start = ((), (), s32[]{:S(2)}) async-start(), calls=%async_computation.10 | async-start | bytes 1081344 | tf_op jit(solution)/shard_map/all_gather | solution.py:61
  483.0 162.5 %all-gather.23.cloned.1.call-start = ((), (), s32[]{:S(2)}) async-start(), calls=%async_computation.11 | async-start | bytes 1081344 | tf_op jit(solution)/shard_map/all_gather | solution.py:61
  483.7 302.0 %reduce-scatter.11.cloned.1.call-start = ((), (), s32[]{:S(2)}) async-start(), calls=%async_computation.15 | async-start | bytes 2162688 | tf_op jit(solution)/shard_map/reduce_scatter | solution.py:64
  488.7 434.1 %reduce-scatter.7.cloned.1.call-start = ((), (), s32[]{:S(2)}) async-start(), calls=%async_computation.13 | async-start | bytes 2162688 | tf_op jit(solution)/shard_map/reduce_scatter | solution.py:64
  543.2 2.0 copy-start.6
  547.9 512.0 %reduce-scatter.9.cloned.1.call-start = ((), (), s32[]{:S(2)}) async-start(), calls=%async_computation.14 | async-start | bytes 2162688 | tf_op jit(solution)/shard_map/reduce_scatter | solution.py:64
  552.8 730.9 %reduce-scatter.5.cloned.1.call-start = ((), (), s32[]{:S(2)}) async-start(), calls=%async_computation.12 | async-start | bytes 21626880 | tf_op jit(solution)/shard_map/reduce_scatter | solution.py:64
  578.9 70.5 %copy-start.3 = (f32[1024]{0:T(1024)S(1)}, f32[1024]{0:T(1024)}, u32[]{:S(2)}) copy-start(f32[1024]{0:T(1024)} %get-tuple-element.23) | copy-start | bytes 12292
  593.9 56.1 %copy-start.1 = (s32[1024]{0:T(1024)S(1)}, s32[1024]{0:T(1024)}, u32[]{:S(2)}) copy-start(s32[1024]{0:T(1024)} %param.9) | copy-start | bytes 12292
Sparse Core Ops, SparseCore 0:
  10.8 88.8 all-gather.8
  102.6 52.3 all-gather.10
  157.9 52.4 all-gather.12
  213.1 52.4 all-gather.14
  377.2 84.9 all-gather.16
  482.3 52.3 all-gather.18
  537.6 52.4 all-gather.20
  593.0 52.4 all-gather.22
  648.3 137.3 reduce-scatter.10
  788.4 134.2 reduce-scatter.6
  925.6 134.2 reduce-scatter.8
  1062.6 221.0 reduce-scatter.4
where the time goes:
time: 1290 us
  waiting for transfers between devices  961 us (74%)
  matrix products  126 us (10%)
  other arithmetic  94.9 us (7%)
  blocking collectives  82.6 us (6%)
  between operations  14.4 us (1%)
    reduce_scatter x4, waiting for transfers between devices, scatter_rows(): return lax.psum_scatter(full_rows, 'fsdp', scatter_dimension=0, tiled=True)  574 us
    all_gather x8, waiting for transfers between devices, gather_rows(): return lax.all_gather(row_shard, 'fsdp', axis=0, tiled=True)  383 us
    psum x1, blocking collectives, device_step(): tok_coef = mask_wide / lax.psum(jnp.sum(mask_wide), 'fsdp')  42.8 us
    convert_element_type x1, other arithmetic, head_forward(): ((exp_rows / sum_exp - is_label.astype(jnp.float32)) * tok_coef[:, None])...  42.4 us
    psum x1, blocking collectives, device_step(): lax.psum(loss_part, 'fsdp')  39.8 us
    dot_general x1, matrix products, head_forward(): lax.dot_general(h_norm, emb_table, ROW_CONTRACT, preferred_element_type=j...  36.6 us
    reduce_sum x1, other arithmetic, head_forward(): sum_exp = jnp.sum(exp_rows, axis=-1, keepdims=True)  27.3 us
    dot_general x1, matrix products, device_step(): lax.dot_general(d_logits, h_norm, TOK_CONTRACT, preferred_element_type=jn...  26 us
  transfers between devices with their start and end apart: 12, of which 12 were waited for; matrix products, arithmetic and copies ran while one was open for 8% of the time, Pallas kernels for 0%

commit v1 on v0

--- a/solution.py
+++ b/solution.py
@@ -1,11 +1,329 @@
+import functools
+
 import jax
 import jax.numpy as jnp
 from jax import lax
+from jax.experimental import pallas as pl
+from jax.experimental.pallas import tpu as pltpu
 from jax.sharding import PartitionSpec as P
 
 NORM_EPS = 1e-6
 ROW_CONTRACT = (((1,), (1,)), ((), ()))
 TOK_CONTRACT = (((0,), (0,)), ((), ()))
+MESH = pl.DeviceIdType.MESH
+N_DEV = 32
+E_ROWS = 640
+W_ROWS = 192
+SPLIT = 416
+CHUNK = 64
+HALF = CHUNK // 2
+E_CHUNKS = E_ROWS // CHUNK
+N_CHUNKS = (E_ROWS + W_ROWS) // CHUNK
+LAG = 2
+PIECES = 4
+ORDER = (3, 0, 1, 2)
+
+
+def dev_index(z, y, x, c):
+    return z * 8 + y * 4 + x * 2 + c
+
+
+def my_coords():
+    me = lax.axis_index("fsdp")
+    return me // 8, (me // 4) % 2, (me // 2) % 2, me % 2
+
+
+def z_partners(z):
+    return (z + 1 - 2 * (z % 2), (z + 2) % 4, 3 - z)
+
+
+def greet(z, y, x, c):
+    barrier = pltpu.get_barrier_semaphore()
+    partners = [dev_index(z, y, x, 1 - c), dev_index(z, y, 1 - x, c), dev_index(z, 1 - y, x, c)]
+    partners += [dev_index(zp, y, x, c) for zp in z_partners(z)]
+    for dev in partners:
+        pl.semaphore_signal(barrier, inc=1, device_id=(dev,), device_id_type=MESH)
+    pl.semaphore_wait(barrier, 6)
+
+
+def gather_kernel(e_ref, w_ref, m_ref, eo_ref, wo_ref, n_ref, tiles, send_sem, recv_sem, own_sem):
+    z, y, x, c = my_coords()
+    me = dev_index(z, y, x, c)
+    zs = (z,) + z_partners(z)
+    greet(z, y, x, c)
+
+    own_src = (e_ref.at[pl.ds(0, SPLIT)], e_ref.at[pl.ds(SPLIT, E_ROWS - SPLIT)], w_ref, m_ref)
+
+    def place(piece, block):
+        if piece == 0:
+            return eo_ref.at[block, pl.ds(0, SPLIT)]
+        if piece == 1:
+            return eo_ref.at[block, pl.ds(SPLIT, E_ROWS - SPLIT)]
+        if piece == 2:
+            return wo_ref.at[block]
+        return tiles.at[block]
+
+    sent = []
+    counts = [0] * PIECES
+
+    def send(piece, block, target, own=False):
+        src = own_src[piece] if own else place(piece, block)
+        copy = pltpu.make_async_remote_copy(src_ref=src, dst_ref=place(piece, block), send_sem=send_sem.at[piece, counts[piece]], recv_sem=recv_sem.at[piece, block], device_id=(target,), device_id_type=MESH)
+        counts[piece] += 1
+        copy.start()
+        sent.append(copy)
+
+    def arrive(piece, block):
+        ref = place(piece, block)
+        pltpu.make_async_copy(ref, ref, recv_sem.at[piece, block]).wait()
+
+    to_core = dev_index(z, y, x, 1 - c)
+    to_x = dev_index(z, y, 1 - x, c)
+    to_y = dev_index(z, 1 - y, x, c)
+    hops = ((to_y, to_x), (to_x, to_y), (to_x, to_y), (to_y, to_x))
+
+    def block_at(piece, depth, k, j=0):
+        if piece in (0, 3):
+            ys, xs = ((y, x), (1 - y, x), ((y, 1 - y)[j], 1 - x))[depth]
+        else:
+            ys, xs = ((y, x), (y, 1 - x), (1 - y, (x, 1 - x)[j]))[depth]
+        return dev_index(zs[k], ys, xs, c)
+
+    for k in (1, 2, 3):
+        for piece in ORDER:
+            send(piece, me, dev_index(zs[k], y, x, c), own=True)
+    for piece in ORDER:
+        send(piece, me, hops[piece][0], own=True)
+    for piece in ORDER:
+        send(piece, me, hops[piece][1], own=True)
+    for piece in ORDER:
+        send(piece, me, to_core, own=True)
+    keep = [pltpu.make_async_copy(own_src[piece], place(piece, me), own_sem.at[piece]) for piece in ORDER]
+    for copy in keep:
+        copy.start()
+
+    for step in range(6):
+        if 1 <= step < 4:
+            for piece in ORDER:
+                block = block_at(piece, 0, step)
+                arrive(piece, block)
+                send(piece, block, hops[piece][0])
+                send(piece, block, hops[piece][1])
+                send(piece, block, to_core)
+        if 1 <= step < 5:
+            for piece in ORDER:
+                block = block_at(piece, 1, step - 1)
+                arrive(piece, block)
+                send(piece, block, hops[piece][1])
+                send(piece, block, to_core)
+        if 2 <= step < 6:
+            for j in range(2):
+                for piece in ORDER:
+                    block = block_at(piece, 2, step - 2, j)
+                    arrive(piece, block)
+                    send(piece, block, to_core)
+    for zb in range(4):
+        for yb in range(2):
+            for xb in range(2):
+                for piece in ORDER:
+                    arrive(piece, dev_index(zb, yb, xb, 1 - c))
+    for copy in sent:
+        copy.wait_send()
+    for copy in keep:
+        copy.wait()
+
+    def total(i, acc):
+        return acc + tiles[i]
+
+    n_ref[...] = lax.fori_loop(0, N_DEV, total, jnp.zeros_like(n_ref))
+
+
+def gather_all(e_shard, w_shard, mask_tile):
+    vmem = pl.BlockSpec(memory_space=pltpu.VMEM)
+    anyspace = pl.BlockSpec(memory_space=pl.ANY)
+    return pl.pallas_call(
+        gather_kernel,
+        out_shape=(jax.ShapeDtypeStruct((N_DEV, E_ROWS, 256), jnp.bfloat16), jax.ShapeDtypeStruct((N_DEV, W_ROWS, 256), jnp.bfloat16), jax.ShapeDtypeStruct((8, 128), jnp.float32)),
+        in_specs=[vmem, vmem, vmem],
+        out_specs=(anyspace, anyspace, vmem),
+        scratch_shapes=[
+            pltpu.VMEM((N_DEV, 8, 128), jnp.float32),
+            pltpu.SemaphoreType.DMA((PIECES, N_DEV)),
+            pltpu.SemaphoreType.DMA((PIECES, N_DEV)),
+            pltpu.SemaphoreType.DMA((PIECES,)),
+        ],
+        compiler_params=pltpu.CompilerParams(collective_id=0, has_side_effects=True),
+        name="gather_all",
+    )(e_shard, w_shard, mask_tile)
+
+
+def scatter_kernel(g_ref, gw_ref, l_ref, out_ref, loss_ref, acc, r0, r1a, r1b, r2, r3, bufs, own_sem, s0, q0, s1, q1, s2, q2, s3, q3, small_send, small_recv):
+    z, y, x, c = my_coords()
+    to_core = dev_index(z, y, x, 1 - c)
+    to_x = dev_index(z, y, 1 - x, c)
+    to_y = dev_index(z, 1 - y, x, c)
+    zs = z_partners(z)
+    greet(z, y, x, c)
+
+    def source(k, core, from_w):
+        if from_w:
+            return gw_ref.at[:, :, :, core, pl.ds((k - E_CHUNKS) * CHUNK, CHUNK)]
+        return g_ref.at[:, :, :, core, pl.ds(k * CHUNK, CHUNK)]
+
+    def remote(src, dst, send_sem, recv_sem, dev):
+        return pltpu.make_async_remote_copy(src_ref=src, dst_ref=dst, send_sem=send_sem, recv_sem=recv_sem, device_id=(dev,), device_id_type=MESH)
+
+    def core_away(k, src):
+        return remote(src, r0.at[k], s0.at[k], q0.at[k], to_core)
+
+    def core_mine(k, src):
+        return pltpu.make_async_copy(src, acc.at[k], own_sem.at[k])
+
+    def plane_first(k):
+        return (
+            remote(acc.at[k, :, :, 1 - x, pl.ds(0, HALF)], r1a.at[k], s1.at[0, k], q1.at[0, k], to_x),
+            remote(acc.at[k, :, 1 - y, :, pl.ds(HALF, HALF)], r1b.at[k], s1.at[1, k], q1.at[1, k], to_y),
+        )
+
+    def plane_second(k):
+        return (
+            remote(r1a.at[k, :, 1 - y], r2.at[k, :, pl.ds(0, HALF)], s2.at[0, k], q2.at[0, k], to_y),
+            remote(r1b.at[k, :, 1 - x], r2.at[k, :, pl.ds(HALF, HALF)], s2.at[1, k], q2.at[1, k], to_x),
+        )
+
+    def along_z(k):
+        return tuple(remote(r2.at[k, zs[i]], r3.at[k, i], s3.at[i, k], q3.at[i, k], dev_index(zs[i], y, x, c)) for i in range(3))
+
+    def begin(from_w):
+        def body(k, carry):
+            core_away(k, source(k, 1 - c, from_w)).start()
+            core_mine(k, source(k, c, from_w)).start()
+            return carry
+
+        return body
+
+    def small(src, slot, dev):
+        return remote(src, bufs.at[slot], small_send.at[slot], small_recv.at[slot], dev)
+
+    small_steps = (
+        (small(l_ref, 0, to_core),),
+        (small(bufs.at[6], 1, to_x),),
+        (small(bufs.at[7], 2, to_y),),
+        tuple(small(bufs.at[8], 3 + i, dev_index(zs[i], y, x, c)) for i in range(3)),
+    )
+    small_steps[0][0].start()
+    lax.fori_loop(0, E_CHUNKS, begin(False), 0)
+    lax.fori_loop(E_CHUNKS, N_CHUNKS, begin(True), 0)
+
+    def step_body(s, carry):
+        @pl.when(s < N_CHUNKS)
+        def _():
+            core_mine(s, acc.at[s]).wait()
+            core_away(s, r0.at[s]).wait_recv()
+
+            def add(i, inner):
+                acc[s, i // 4, (i // 2) % 2, i % 2] += r0[s, i // 4, (i // 2) % 2, i % 2]
+                return inner
+
+            lax.fori_loop(0, 16, add, 0)
+            for copy in plane_first(s):
+                copy.start()
+
+        @pl.when((s >= LAG) & (s < N_CHUNKS + LAG))
+        def _():
+            k = s - LAG
+            for copy in plane_first(k):
+                copy.wait_recv()
+
+            def add(i, inner):
+                r1a[k, i // 2, i % 2] += acc[k, i // 2, i % 2, x, pl.ds(0, HALF)]
+                r1b[k, i // 2, i % 2] += acc[k, i // 2, y, i % 2, pl.ds(HALF, HALF)]
+                return inner
+
+            lax.fori_loop(0, 8, add, 0)
+            for copy in plane_second(k):
+                copy.start()
+
+        @pl.when((s >= 2 * LAG) & (s < N_CHUNKS + 2 * LAG))
+        def _():
+            k = s - 2 * LAG
+            for copy in plane_second(k):
+                copy.wait_recv()
+
+            def add(i, inner):
+                r2[k, i, pl.ds(0, HALF)] += r1a[k, i, y]
+                r2[k, i, pl.ds(HALF, HALF)] += r1b[k, i, x]
+                return inner
+
+            lax.fori_loop(0, 4, add, 0)
+            for copy in along_z(k):
+                copy.start()
+
+        @pl.when(s >= 3 * LAG)
+        def _():
+            k = s - 3 * LAG
+            for copy in along_z(k):
+                copy.wait_recv()
+            out_ref[k] = (r2[k, z] + r3[k, 0]) + (r3[k, 1] + r3[k, 2])
+
+        for i in range(3):
+
+            @pl.when(s == 1 + 3 * i)
+            def _():
+                small_steps[i][0].wait()
+                bufs[6 + i] = (l_ref[...] if i == 0 else bufs[5 + i]) + bufs[i]
+                for copy in small_steps[i + 1]:
+                    copy.start()
+
+        return carry
+
+    lax.fori_loop(0, N_CHUNKS + 3 * LAG, step_body, 0)
+
+    for copy in small_steps[3]:
+        copy.wait()
+    loss_ref[...] = (bufs[8] + bufs[3]) + (bufs[4] + bufs[5])
+
+    def finish(k, carry):
+        core_away(k, r0.at[k]).wait_send()
+        for copy in plane_first(k) + plane_second(k) + along_z(k):
+            copy.wait_send()
+        return carry
+
+    lax.fori_loop(0, N_CHUNKS, finish, 0)
+
+
+def scatter_all(grad_blocks, weight_blocks, loss_tile):
+    vmem = pl.BlockSpec(memory_space=pltpu.VMEM)
+    anyspace = pl.BlockSpec(memory_space=pl.ANY)
+    dma = pltpu.SemaphoreType.DMA
+    return pl.pallas_call(
+        scatter_kernel,
+        out_shape=(jax.ShapeDtypeStruct((N_CHUNKS, CHUNK, 256), jnp.float32), jax.ShapeDtypeStruct((8, 128), jnp.float32)),
+        in_specs=[anyspace, anyspace, vmem],
+        out_specs=(vmem, vmem),
+        scratch_shapes=[
+            pltpu.VMEM((N_CHUNKS, 4, 2, 2, CHUNK, 256), jnp.float32),
+            pltpu.VMEM((N_CHUNKS, 4, 2, 2, CHUNK, 256), jnp.float32),
+            pltpu.VMEM((N_CHUNKS, 4, 2, HALF, 256), jnp.float32),
+            pltpu.VMEM((N_CHUNKS, 4, 2, HALF, 256), jnp.float32),
+            pltpu.VMEM((N_CHUNKS, 4, CHUNK, 256), jnp.float32),
+            pltpu.VMEM((N_CHUNKS, 3, CHUNK, 256), jnp.float32),
+            pltpu.VMEM((9, 8, 128), jnp.float32),
+            dma((N_CHUNKS,)),
+            dma((N_CHUNKS,)),
+            dma((N_CHUNKS,)),
+            dma((2, N_CHUNKS)),
+            dma((2, N_CHUNKS)),
+            dma((2, N_CHUNKS)),
+            dma((2, N_CHUNKS)),
+            dma((3, N_CHUNKS)),
+            dma((3, N_CHUNKS)),
+            dma((6,)),
+            dma((6,)),
+        ],
+        compiler_params=pltpu.CompilerParams(collective_id=1, has_side_effects=True, vmem_limit_bytes=60 * 1024 * 1024),
+        name="scatter_all",
+    )(grad_blocks, weight_blocks, loss_tile)
 
 
 def rms_scale(rows_wide, norm_gain):
@@ -56,35 +374,36 @@
     return grad_x, grad_gate, grad_up, grad_down
 
 
+def rows_to_tiles(rows):
+    return rows.reshape(-1, 8, 8, 256).transpose(0, 2, 1, 3).reshape(-1, 64, 256)
+
+
+def tiles_to_rows(tiles):
+    return tiles.reshape(-1, 8, 8, 256).transpose(0, 2, 1, 3).reshape(-1, 2048)
+
+
 def solution(mesh):
-    def gather_rows(row_shard):
-        return lax.all_gather(row_shard, "fsdp", axis=0, tiled=True)
-
-    def scatter_rows(full_rows):
-        return lax.psum_scatter(full_rows, "fsdp", scatter_dimension=0, tiled=True)
-
     def device_step(tok_ids, tok_labels, loss_mask, table_shard, gain_mlp, gain_head, gate_shard, up_shard, down_shard):
         mask_wide = loss_mask.astype(jnp.float32)
-        tok_coef = mask_wide / lax.psum(jnp.sum(mask_wide), "fsdp")
-        table_full = gather_rows(table_shard)
-        gate_full = gather_rows(gate_shard)
-        up_full = gather_rows(up_shard)
-        down_full = gather_rows(down_shard)
+        w_shard = jnp.concatenate([rows_to_tiles(gate_shard)[0], rows_to_tiles(up_shard)[0], down_shard], axis=0)
+        table_blocks, w_blocks, mask_total = gather_all(table_shard, w_shard, jnp.broadcast_to(jnp.sum(mask_wide), (8, 128)))
+        tok_coef = mask_wide / mask_total[0, 0]
+        table_full = table_blocks.reshape(-1, 256)
+        gate_full = tiles_to_rows(w_blocks[:, 0:64])
+        up_full = tiles_to_rows(w_blocks[:, 64:128])
+        down_full = w_blocks[:, 128:192].reshape(-1, 256)
         emb_rows = jnp.take(table_full, tok_ids, axis=0)
         saved, h_norm = mlp_forward(emb_rows, gain_mlp, gain_head, gate_full, up_full, down_full)
         loss_part, d_logits = head_forward(h_norm, table_full, tok_labels, tok_coef)
-        table_again, d_logits = lax.optimization_barrier((table_shard, d_logits))
-        table_back = gather_rows(table_again)
-        d_hnorm = jnp.dot(d_logits, table_back, preferred_element_type=jnp.float32)
+        d_hnorm = jnp.dot(d_logits, table_full, preferred_element_type=jnp.float32)
         head_grad = lax.dot_general(d_logits, h_norm, TOK_CONTRACT, preferred_element_type=jnp.float32)
         d_hidden = rms_back(saved[7], saved[8], gain_head, d_hnorm)
-        gate_again, up_again, down_again, d_hidden = lax.optimization_barrier((gate_shard, up_shard, down_shard, d_hidden))
-        gate_back = gather_rows(gate_again)
-        up_back = gather_rows(up_again)
-        down_back = gather_rows(down_again)
-        grad_x, grad_gate, grad_up, grad_down = mlp_backward(saved, d_hidden, gain_mlp, gate_back, up_back, down_back)
-        grad_table = head_grad + jax.ops.segment_sum(grad_x, tok_ids, num_segments=table_back.shape[0])
-        return (lax.psum(loss_part, "fsdp"), scatter_rows(grad_table), scatter_rows(grad_gate), scatter_rows(grad_up), scatter_rows(grad_down))
+        grad_x, grad_gate, grad_up, grad_down = mlp_backward(saved, d_hidden, gain_mlp, gate_full, up_full, down_full)
+        grad_table = head_grad + jax.ops.segment_sum(grad_x, tok_ids, num_segments=table_full.shape[0])
+        grad_w = jnp.concatenate([rows_to_tiles(grad_gate), rows_to_tiles(grad_up), grad_down.reshape(-1, 64, 256)], axis=1)
+        out, loss = scatter_all(grad_table.reshape(4, 2, 2, 2, E_ROWS, 256), grad_w.reshape(4, 2, 2, 2, W_ROWS, 256), jnp.broadcast_to(loss_part, (8, 128)))
+        g_tab = out[:E_CHUNKS].reshape(E_ROWS, 256)
+        return loss[0, 0], g_tab, tiles_to_rows(out[E_CHUNKS]), tiles_to_rows(out[E_CHUNKS + 1]), out[E_CHUNKS + 2]
 
     row_spec = P("fsdp", None)
     tok_spec = P("fsdp")

time: 1290 us -> 441 us (0.34)
  waiting for transfers between devices: 961 us -> 0 us
  Pallas kernels: 0 us -> 207 us
  blocking collectives: 82.6 us -> 0 us
  matrix products: 126 us -> 105 us
  between operations: 14.4 us -> 0.91 us
    reduce_scatter x4 -> x0, waiting for transfers between devices: 574 us -> none  [scatter_rows(): return lax.psum_scatter(full_rows, 'fsdp', scatter_dimension=0, tiled=True)]
    all_gather x8 -> x0, waiting for transfers between devices: 383 us -> none  [gather_rows(): return lax.all_gather(row_shard, 'fsdp', axis=0, tiled=True)]
    pallas_call x0 -> x2, Pallas kernels: none -> 207 us  [the longest x1 133 us: scatter_all(): pl.pallas_call(scatter_kernel, out_shape=(jax.ShapeDtypeStruct((N_CHUNKS,...]
    psum x2 -> x0, blocking collectives: 82.6 us -> none  [the longest x1 42.8 us: device_step(): tok_coef = mask_wide / lax.psum(jnp.sum(mask_wide), 'fsdp')]
  transfers between devices with their start and end apart: 12 -> 0, of which waited for: 12 -> 0; matrix products, arithmetic and copies ran while one was open for 8% -> 0% of each run, Pallas kernels for 0% -> 0%
where the time goes in v1:
time: 441 us; the launch traced here: 440 us
  Pallas kernels  207 us (47%)
  other arithmetic  106 us (24%)
  matrix products  105 us (24%)
  local copies, waits for them, and re-layouts  21.7 us (5%)
    pallas_call x1, Pallas kernels, scatter_all(): pl.pallas_call(scatter_kernel, out_shape=(jax.ShapeDtypeStruct((N_CHUNKS,...  133 us
    pallas_call x1, Pallas kernels, gather_all(): pl.pallas_call(gather_kernel, out_shape=(jax.ShapeDtypeStruct((N_DEV, E_R...  73.4 us
    convert_element_type x1, other arithmetic, head_forward(): ((exp_rows / sum_exp - is_label.astype(jnp.float32)) * tok_coef[:, None])...  42.3 us
    dot_general x1, matrix products, head_forward(): lax.dot_general(h_norm, emb_table, ROW_CONTRACT, preferred_element_type=j...  36.6 us
    reduce_sum x1, other arithmetic, head_forward(): picked = jnp.sum(jnp.where(is_label, logits, 0.0), axis=-1)  31.5 us
    dot_general x1, matrix products, device_step(): lax.dot_general(d_logits, h_norm, TOK_CONTRACT, preferred_element_type=jn...  26 us
    scatter-add x1, other arithmetic, device_step(): jax.ops.segment_sum(grad_x, tok_ids, num_segments=table_full.shape[0])  20.1 us
    dot_general x1, matrix products, device_step(): d_hnorm = jnp.dot(d_logits, table_full, preferred_element_type=jnp.float32)  19.7 us

profile of v1, /device:TPU:0, one launch (start us, length us, event | category | flops | bytes accessed | tf_op | source)
XLA Modules:
  0.0 440.4 jit_solution(7312677390436179368)
XLA Ops:
  0.6 0.0 copy-start.14
  0.6 1.3 convert_reduce_fusion
  1.9 0.7 compare_and_fusion
  2.6 1.2 broadcast_in_dim.23.m_ref
  3.9 0.7 fusion.33
  4.6 1.4 pad_maximum_fusion.1.w_ref
  6.0 73.4 %gather_all.1 = (bf16[32,640,256]{2,1,0:T(8,128)(2,1)}, bf16[32,192,256]{2,1,0:T(8,128)(2,1)}, f32[8,128]{1,0:T(8,128)}) custom-call(bf16[640,256]{1,0:T(8,128)(2,1)} %e_ref.1, bf16[192,256]{1,0:T(8,128)(2,1)} %pad_maximum_fusion.1.w_ref, f32[8,128]{1,0:T(8,128)} %broadcast_in_dim.23.m_ref), custom_call_target="tpu_custom_call" | custom-call | tf_op jit(solution)/shard_map/gather_all/pallas_call | solution.py:144
  79.4 1.2 slice.30
  80.6 8.8 %gather_fusion = bf16[1024,256]{1,0:T(8,128)(2,1)S(1)} fusion(bf16[20480,256]{1,0:T(8,128)(2,1)} %bitcast.68, s32[1024]{0:T(1024)S(1)} %fusion.33), kind=kCustom, calls=%fused_computation | custom fusion | bytes 1052672 | tf_op jit(solution)/shard_map/jit(_take)/gather | solution.py:395
  89.4 0.2 copy.15
  89.6 0.2 fusion.20
  89.8 0.6 fusion.34
  90.4 2.1 fusion.42
  92.5 0.0 copy-start.2
  92.6 0.0 copy-start.5
  92.6 1.0 copy-done.2
  93.5 0.0 copy-done.14
  93.5 1.4 convolution_convert_fusion.1
  94.9 0.0 copy-start
  94.9 4.5 %fusion.1 = (bf16[1024,2048]{1,0:T(8,128)(2,1)S(1)}, bf16[1024,2048]{1,0:T(8,128)(2,1)}) fusion(bf16[1024,2048]{1,0:T(8,128)(2,1)S(1)} %convolution_convert_fusion.1, bf16[256,2048]{1,0:T(8,128)(2,1)S(1)} %bitcast.76, f32[256]{0:T(256)S(1)} %copy-done.14, f32[1024]{0:T(1024)S(1)} %get-tuple-element.28, bf16[1024,256]{0,1:T(8,128)(2,1)S(1)} %copy.15, ...), kind=kOutput, calls=%fused_computation.13 | convolution fusion | flops 1093926912 | bytes 14161920 | tf_op jit(solution)/shard_map/dot_general | solution.py:343
  99.4 0.0 copy-done.7
  99.4 0.0 copy-done.5
  99.4 0.0 copy-done
  99.5 0.0 copy-start.16
  99.5 0.0 copy-start.9
  99.5 1.3 fusion.13
  100.8 0.7 copy-done.16
  101.5 0.0 copy-done.9
  101.5 36.6 %fusion.43 = (f32[1024]{0:T(1024)S(1)}, f32[1024,20480]{1,0:T(8,128)}) fusion(bf16[20480,256]{1,0:T(8,128)(2,1)} %bitcast.69, bf16[1024,256]{0,1:T(8,128)(2,1)S(1)} %get-tuple-element.34, f32[256]{0:T(256)S(1)} %copy-done.9, f32[1024]{0:T(1024)S(1)} %get-tuple-element.30), kind=kOutput, calls=%fused_computation.75 | convolution fusion | flops 10759437312 | bytes 94905344 | tf_op jit(solution)/shard_map/dot_general | solution.py:352
  138.1 0.0 copy-done.11
  138.1 31.5 %select_reduce_fusion = (f32[1024]{0:T(1024)S(1)}, f32[1024]{0:T(1024)S(1)}) fusion(f32[1024,20480]{1,0:T(8,128)} %get-tuple-element.36, s32[1024]{0:T(1024)S(1)} %copy-done.11, f32[1024]{0:T(1024)S(1)} %get-tuple-element.35), kind=kLoop, calls=%fused_computation.2 | loop fusion | flops 104855552 | bytes 83902464 | tf_op jit(solution)/shard_map/reduce_sum | solution.py:357
  169.7 0.0 copy-done.13
  169.7 1.3 multiply_reduce_fusion
  170.9 42.3 %multiply_convert_fusion = bf16[1024,20480]{1,0:T(8,128)(2,1)} fusion(f32[1024,20480]{1,0:T(8,128)} %get-tuple-element.36, f32[1024]{0:T(1024)S(1)} %get-tuple-element.18, s32[1024]{0:T(1024)S(1)} %copy-done.11, f32[1024]{0:T(1024)S(1)} %get-tuple-element.16, f32[1024]{0:T(1024)S(1)} %get-tuple-element.35), kind=kLoop, calls=%fused_computation.3 | loop fusion | flops 146800640 | bytes 125845504 | tf_op jit(solution)/shard_map/convert_element_type | solution.py:359
  213.2 19.7 %fusion.19 = (f32[1024]{0:T(1024)S(1)}, f32[1024,256]{0,1:T(8,128)S(1)}) fusion(bf16[1024,256]{0,1:T(8,128)(2,1)S(1)} %get-tuple-element.34, f32[256]{0:T(256)S(1)} %copy-done.9, bf16[1024,20480]{1,0:T(8,128)(2,1)} %multiply_convert_fusion, bf16[20480,256]{1,0:T(8,128)(2,1)} %bitcast.70), kind=kOutput, calls=%fused_computation.45 | convolution fusion | flops 10738465792 | bytes 54006784 | tf_op jit(solution)/shard_map/dot_general | solution.py:398
  232.9 0.0 copy-start.17
  232.9 26.0 %fusion.29 = f32[20480,256]{1,0:T(8,128)} fusion(bf16[1024,20480]{1,0:T(8,128)(2,1)} %multiply_convert_fusion, bf16[1024,256]{0,1:T(8,128)(2,1)S(1)} %get-tuple-element.34, f32[256]{0:T(256)S(1)} %copy-done.9, f32[1024]{0:T(1024)S(1)} %get-tuple-element.30), kind=kOutput, calls=%fused_computation.56 | convolution fusion | flops 10738466816 | bytes 63443968 | tf_op jit(solution)/shard_map/dot_general | solution.py:399
  258.9 1.4 broadcast_in_dim.45.l_ref
  260.3 0.2 fusion.28
  260.5 0.0 copy-done.17
  260.5 2.7 fusion.45
  263.2 0.0 copy-done.1
  263.2 0.0 copy-done.18
  263.2 0.0 copy-start.15
  263.3 4.8 %fusion.10 = (bf16[1024,2048]{1,0:T(8,128)(2,1)S(1)}, bf16[1024,2048]{1,0:T(8,128)(2,1)S(1)}) fusion(bf16[1024,2048]{1,0:T(8,128)(2,1)S(1)} %copy-done.1, bf16[1024,2048]{1,0:T(8,128)(2,1)S(1)} %copy-done.18, bf16[1024,256]{0,1:T(8,128)(2,1)S(1)} %fusion.28, bf16[2048,256]{1,0:T(8,128)(2,1)S(1)} %bitcast.79), kind=kOutput, calls=%fused_computation.22 | convolution fusion | flops 1105199104 | bytes 18350080 | tf_op jit(solution)/shard_map/dot_general | solution.py:366
  268.1 0.0 copy-start.6
  268.1 0.0 copy-done.3
  268.1 1.3 fusion.44
  269.4 0.0 copy-done.8
  269.4 2.6 fusion.38
  272.1 0.0 copy-done.6
  272.1 1.4 fusion.27
  273.4 0.0 copy-start.10
  273.5 2.7 fusion.36
  276.1 0.5 fusion.26
  276.6 0.3 copy.16
  276.9 0.0 copy-done.10
  276.9 0.0 copy-start.4
  276.9 20.1 %scatter_fusion = f32[20480,256]{1,0:T(8,128)} fusion(f32[20480,256]{1,0:T(8,128)} %fusion.29, s32[1024]{0:T(1024)S(1)} %copy-done.10, f32[1024,256]{1,0:T(8,128)S(1)} %copy.16), kind=kCustom, calls=%fused_computation.1 | custom fusion | flops 262144 | bytes 3149824 | tf_op jit(solution)/shard_map/scatter-add | solution.py:402
  297.0 5.5 %pad_maximum_fusion.gw_ref = f32[4,2,2,2,192,256]{5,4,3,2,1,0:T(8,128)} fusion(f32[4,2,2,2,64,256]{5,4,3,2,1,0:T(8,128)S(1)} %bitcast.73, f32[4,2,2,2,64,256]{5,4,3,2,1,0:T(8,128)} %bitcast.75, f32[4,2,2,2,64,256]{5,4,3,2,1,0:T(8,128)} %bitcast.74), kind=kLoop, calls=%fused_computation.23 | loop fusion | flops 3145728 | bytes 12582912 | tf_op jit(solution)/shard_map/concatenate | solution.py:403
  302.5 133.2 %scatter_all.1 = (f32[13,64,256]{2,1,0:T(8,128)}, f32[8,128]{1,0:T(8,128)}) custom-call(f32[4,2,2,2,640,256]{5,4,3,2,1,0:T(8,128)} %bitcast.67, f32[4,2,2,2,192,256]{5,4,3,2,1,0:T(8,128)} %pad_maximum_fusion.gw_ref, f32[8,128]{1,0:T(8,128)} %broadcast_in_dim.45.l_ref), custom_call_target="tpu_custom_call" | custom-call | tf_op jit(solution)/shard_map/scatter_all/pallas_call | solution.py:299
  435.7 1.2 slice.31
  436.9 1.6 slice_bitcast_fusion
  438.4 2.0 slice.32
  (14 shorter events, 0.0 us)
Async XLA Ops:
  0.6 92.9 %copy-start.14 = (f32[256]{0:T(256)S(1)}, f32[256]{0:T(256)}, u32[]{:S(2)}) copy-start(f32[256]{0:T(256)} %param.13) | copy-start | bytes 3076
  90.4 9.1 %copy-start.7 = (f32[1024]{0:T(1024)}, f32[1024]{0:T(1024)S(1)}, u32[]{:S(2)}) copy-start(f32[1024]{0:T(1024)S(1)} %get-tuple-element.28) | copy-start | bytes 12292
  92.5 1.0 copy-start.2
  92.6 6.9 %copy-start.5 = (bf16[32,64,256]{2,1,0:T(8,128)(2,1)}, bf16[32,64,256]{2,1,0:T(8,128)(2,1)S(1)}, u32[]{:S(2)}) copy-start(bf16[32,64,256]{2,1,0:T(8,128)(2,1)S(1)} %get-tuple-element.22) | copy-start | bytes 3145732
  94.9 4.5 %copy-start = (bf16[1024,2048]{1,0:T(8,128)(2,1)}, bf16[1024,2048]{1,0:T(8,128)(2,1)S(1)}, u32[]{:S(2)}) copy-start(bf16[1024,2048]{1,0:T(8,128)(2,1)S(1)} %convolution_convert_fusion.1) | copy-start | bytes 12582916
  99.5 2.1 copy-start.16
  99.5 2.1 copy-start.9
  101.5 36.6 %copy-start.11 = (s32[1024]{0:T(1024)S(1)}, s32[1024]{0:T(1024)}, u32[]{:S(2)}) copy-start(s32[1024]{0:T(1024)} %param.10) | copy-start | bytes 12292
  138.1 31.5 %copy-start.13 = (s32[1024]{0:T(1024)S(1)}, s32[1024]{0:T(1024)}, u32[]{:S(2)}) copy-start(s32[1024]{0:T(1024)} %param.11) | copy-start | bytes 12292
  232.9 27.6 %copy-start.17 = (bf16[1024,2048]{1,0:T(8,128)(2,1)S(1)}, bf16[1024,2048]{1,0:T(8,128)(2,1)}, u32[]{:S(2)}) copy-start(bf16[1024,2048]{1,0:T(8,128)(2,1)} %copy-done.16) | copy-start | bytes 12582916
  258.9 4.3 copy-start.1
  258.9 4.3 copy-start.18
  263.2 4.9 %copy-start.3 = (bf16[32,64,256]{2,1,0:T(8,128)(2,1)S(1)}, bf16[32,64,256]{2,1,0:T(8,128)(2,1)}, u32[]{:S(2)}) copy-start(bf16[32,64,256]{2,1,0:T(8,128)(2,1)} %copy-done.2) | copy-start | bytes 3145732
  263.2 6.2 %copy-start.8 = (f32[1024]{0:T(1024)S(1)}, f32[1024]{0:T(1024)}, u32[]{:S(2)}) copy-start(f32[1024]{0:T(1024)} %copy-done.7) | copy-start | bytes 12292
  263.2 6.2 %copy-start.15 = (f32[256]{0:T(256)S(1)}, f32[256]{0:T(256)}, u32[]{:S(2)}) copy-start(f32[256]{0:T(256)} %param.13) | copy-start | bytes 3076
  268.1 4.0 copy-start.6
  272.1 4.1 copy-start.12
  273.4 3.5 copy-start.10
  276.9 20.1 %copy-start.4 = (f32[2048,256]{1,0:T(8,128)S(1)}, f32[2048,256]{1,0:T(8,128)}, u32[]{:S(2)}) copy-start(f32[2048,256]{1,0:T(8,128)} %fusion.45) | copy-start | bytes 6291460

commit v2 on v1

--- a/solution.py
+++ b/solution.py
@@ -20,6 +20,13 @@
 E_CHUNKS = E_ROWS // CHUNK
 N_CHUNKS = (E_ROWS + W_ROWS) // CHUNK
 LAG = 2
+AHEAD = 2
+W_CHUNKS = 3
+LOG2E = 1.4426950408889634
+LN2 = 0.6931471805599453
+VOCAB_TILE = 2048
+UNIT = 512
+TOK_TILE = 256
 PIECES = 4
 ORDER = (3, 0, 1, 2)
 
@@ -157,7 +164,7 @@
     )(e_shard, w_shard, mask_tile)
 
 
-def scatter_kernel(g_ref, gw_ref, l_ref, out_ref, loss_ref, acc, r0, r1a, r1b, r2, r3, bufs, own_sem, s0, q0, s1, q1, s2, q2, s3, q3, small_send, small_recv):
+def scatter_kernel(dl_ref, hn_ref, dx_ref, id_ref, gg_ref, gu_ref, gd_ref, l_ref, out_ref, loss_ref, acc, r0, r1a, r1b, r2, r3, bufs, dl_buf, away_buf, hot, own_sem, load_sem, s0, q0, s1, q1, s2, q2, s3, q3, small_send, small_recv):
     z, y, x, c = my_coords()
     to_core = dev_index(z, y, x, 1 - c)
     to_x = dev_index(z, y, 1 - x, c)
@@ -165,19 +172,52 @@
     zs = z_partners(z)
     greet(z, y, x, c)
 
-    def source(k, core, from_w):
-        if from_w:
-            return gw_ref.at[:, :, :, core, pl.ds((k - E_CHUNKS) * CHUNK, CHUNK)]
-        return g_ref.at[:, :, :, core, pl.ds(k * CHUNK, CHUNK)]
-
     def remote(src, dst, send_sem, recv_sem, dev):
         return pltpu.make_async_remote_copy(src_ref=src, dst_ref=dst, send_sem=send_sem, recv_sem=recv_sem, device_id=(dev,), device_id_type=MESH)
 
     def core_away(k, src):
         return remote(src, r0.at[k], s0.at[k], q0.at[k], to_core)
 
-    def core_mine(k, src):
-        return pltpu.make_async_copy(src, acc.at[k], own_sem.at[k])
+    def load(k):
+        slot = k % 2
+        return pltpu.make_async_copy(dl_ref.at[:, :, :, :, pl.ds((k - W_CHUNKS) * CHUNK, CHUNK)], dl_buf.at[slot], load_sem.at[slot])
+
+    def table_rows(k):
+        slot = k % 2
+        load(k).wait()
+
+        @pl.when(k >= W_CHUNKS + 2)
+        def _():
+            core_away(k - 2, away_buf.at[slot]).wait_send()
+
+        row = lax.broadcasted_iota(jnp.int32, (CHUNK, id_ref.shape[1]), 0)
+        hn = hn_ref[...]
+        dx = dx_ref[...]
+        for mine in range(2):
+            core = c if mine else 1 - c
+
+            def part(zp, carry, mine=mine, core=core):
+                for i in range(8):
+                    dev = dev_index(2 * zp + i // 4, (i // 2) % 2, i % 2, core)
+                    here = row == id_ref[...] - (dev * E_ROWS + (k - W_CHUNKS) * CHUNK)
+                    hot[i * CHUNK : (i + 1) * CHUNK] = jnp.where(here, 1.0, 0.0).astype(jnp.bfloat16)
+                head = jnp.dot(dl_buf[slot, pl.ds(2 * zp, 2), :, :, core].reshape(8 * CHUNK, -1), hn, preferred_element_type=jnp.float32)
+                rows = jnp.dot(hot[...], dx, preferred_element_type=jnp.float32)
+                rows = rows[:, 0:256] + (rows[:, 256:512] + rows[:, 512:768])
+                total = (head + 2.0 * rows).reshape(2, 2, 2, CHUNK, 256)
+                if mine:
+                    acc[k, pl.ds(2 * zp, 2)] = total
+                else:
+                    away_buf[slot, pl.ds(2 * zp, 2)] = total
+                return carry
+
+            lax.fori_loop(0, 2, part, 0)
+            if not mine:
+                core_away(k, away_buf.at[slot]).start()
+
+        @pl.when(k + 2 < N_CHUNKS)
+        def _():
+            load(k + 2).start()
 
     def plane_first(k):
         return (
@@ -193,14 +233,6 @@
 
     def along_z(k):
         return tuple(remote(r2.at[k, zs[i]], r3.at[k, i], s3.at[i, k], q3.at[i, k], dev_index(zs[i], y, x, c)) for i in range(3))
-
-    def begin(from_w):
-        def body(k, carry):
-            core_away(k, source(k, 1 - c, from_w)).start()
-            core_mine(k, source(k, c, from_w)).start()
-            return carry
-
-        return body
 
     def small(src, slot, dev):
         return remote(src, bufs.at[slot], small_send.at[slot], small_recv.at[slot], dev)
@@ -212,13 +244,24 @@
         tuple(small(bufs.at[8], 3 + i, dev_index(zs[i], y, x, c)) for i in range(3)),
     )
     small_steps[0][0].start()
-    lax.fori_loop(0, E_CHUNKS, begin(False), 0)
-    lax.fori_loop(E_CHUNKS, N_CHUNKS, begin(True), 0)
+    w_refs = (gg_ref, gu_ref, gd_ref)
+    for k in range(W_CHUNKS):
+        core_away(k, w_refs[k].at[:, :, :, 1 - c]).start()
+        pltpu.make_async_copy(w_refs[k].at[:, :, :, c], acc.at[k], own_sem.at[k]).start()
+    for k in range(W_CHUNKS, W_CHUNKS + 2):
+        load(k).start()
 
     def step_body(s, carry):
+        @pl.when((s + AHEAD >= W_CHUNKS) & (s + AHEAD < N_CHUNKS))
+        def _():
+            table_rows(s + AHEAD)
+
+        @pl.when(s < W_CHUNKS)
+        def _():
+            pltpu.make_async_copy(acc.at[s], acc.at[s], own_sem.at[s]).wait()
+
         @pl.when(s < N_CHUNKS)
         def _():
-            core_mine(s, acc.at[s]).wait()
             core_away(s, r0.at[s]).wait_recv()
 
             def add(i, inner):
@@ -283,8 +326,10 @@
         copy.wait()
     loss_ref[...] = (bufs[8] + bufs[3]) + (bufs[4] + bufs[5])
 
+    for k in (*range(W_CHUNKS), N_CHUNKS - 2, N_CHUNKS - 1):
+        core_away(k, r0.at[k]).wait_send()
+
     def finish(k, carry):
-        core_away(k, r0.at[k]).wait_send()
         for copy in plane_first(k) + plane_second(k) + along_z(k):
             copy.wait_send()
         return carry
@@ -292,14 +337,16 @@
     lax.fori_loop(0, N_CHUNKS, finish, 0)
 
 
-def scatter_all(grad_blocks, weight_blocks, loss_tile):
+def scatter_all(d_logits_t, h_norm, dx_parts, tok_ids, grad_gate, grad_up, grad_down, loss_tile):
     vmem = pl.BlockSpec(memory_space=pltpu.VMEM)
     anyspace = pl.BlockSpec(memory_space=pl.ANY)
     dma = pltpu.SemaphoreType.DMA
+    n_tok = h_norm.shape[0]
+    mesh_rows = (4, 2, 2, 2)
     return pl.pallas_call(
         scatter_kernel,
         out_shape=(jax.ShapeDtypeStruct((N_CHUNKS, CHUNK, 256), jnp.float32), jax.ShapeDtypeStruct((8, 128), jnp.float32)),
-        in_specs=[anyspace, anyspace, vmem],
+        in_specs=[anyspace, vmem, vmem, vmem, anyspace, anyspace, anyspace, vmem],
         out_specs=(vmem, vmem),
         scratch_shapes=[
             pltpu.VMEM((N_CHUNKS, 4, 2, 2, CHUNK, 256), jnp.float32),
@@ -309,7 +356,11 @@
             pltpu.VMEM((N_CHUNKS, 4, CHUNK, 256), jnp.float32),
             pltpu.VMEM((N_CHUNKS, 3, CHUNK, 256), jnp.float32),
             pltpu.VMEM((9, 8, 128), jnp.float32),
-            dma((N_CHUNKS,)),
+            pltpu.VMEM((2, *mesh_rows, CHUNK, n_tok), jnp.bfloat16),
+            pltpu.VMEM((2, 4, 2, 2, CHUNK, 256), jnp.float32),
+            pltpu.VMEM((8 * CHUNK, n_tok), jnp.bfloat16),
+            dma((W_CHUNKS,)),
+            dma((2,)),
             dma((N_CHUNKS,)),
             dma((N_CHUNKS,)),
             dma((2, N_CHUNKS)),
@@ -321,9 +372,9 @@
             dma((6,)),
             dma((6,)),
         ],
-        compiler_params=pltpu.CompilerParams(collective_id=1, has_side_effects=True, vmem_limit_bytes=60 * 1024 * 1024),
+        compiler_params=pltpu.CompilerParams(collective_id=1, has_side_effects=True, vmem_limit_bytes=63 * 1024 * 1024),
         name="scatter_all",
-    )(grad_blocks, weight_blocks, loss_tile)
+    )(d_logits_t.reshape(*mesh_rows, E_ROWS, n_tok), h_norm, dx_parts, tok_ids, *(g.reshape(*mesh_rows, 64, 256) for g in (grad_gate, grad_up, grad_down)), loss_tile)
 
 
 def rms_scale(rows_wide, norm_gain):
@@ -348,16 +399,98 @@
     return (emb_wide, inv_first, a_norm, gate_wide, up_wide, gate_sig, act_rows, hid_wide, inv_second), h_norm
 
 
-def head_forward(h_norm, emb_table, tok_labels, tok_coef):
-    logits = lax.dot_general(h_norm, emb_table, ROW_CONTRACT, preferred_element_type=jnp.float32)
-    row_max = jnp.max(logits, axis=-1, keepdims=True)
-    exp_rows = jnp.exp(logits - row_max)
-    sum_exp = jnp.sum(exp_rows, axis=-1, keepdims=True)
-    is_label = jnp.arange(logits.shape[1])[None, :] == tok_labels[:, None]
-    picked = jnp.sum(jnp.where(is_label, logits, 0.0), axis=-1)
-    tok_loss = row_max[:, 0] + jnp.log(sum_exp[:, 0]) - picked
-    d_logits = ((exp_rows / sum_exp - is_label.astype(jnp.float32)) * tok_coef[:, None]).astype(jnp.bfloat16)
-    return jnp.sum(tok_coef * tok_loss), d_logits
+def head_kernel(ht_ref, e_ref, lab_ref, coef_ref, dl_ref, dhn_ref, loss_ref, m_s, s_s, pick_s, bias_s):
+    phase, j = pl.program_id(0), pl.program_id(1)
+    n_tok = ht_ref.shape[1]
+    n_tiles = pl.num_programs(1)
+    vt, ur, tb = VOCAB_TILE, UNIT, TOK_TILE
+    units = [(b, r) for b in range(n_tok // tb) for r in range(vt // ur)]
+
+    def scaled(unit):
+        b, r = unit
+        return jnp.dot(e_ref[r * ur : (r + 1) * ur], ht_ref[:, b * tb : (b + 1) * tb], preferred_element_type=jnp.float32)
+
+    def pipeline(process):
+        ahead = scaled(units[0])
+        for i, unit in enumerate(units):
+            now = ahead
+            if i + 1 < len(units):
+                ahead = scaled(units[i + 1])
+            process(unit, now.reshape(ur // 8, 8, tb))
+
+    @pl.when(phase == 0)
+    def _():
+        @pl.when(j == 0)
+        def _():
+            m_s[...] = jnp.full_like(m_s, -jnp.inf)
+            s_s[...] = jnp.zeros_like(s_s)
+            pick_s[...] = jnp.zeros_like(pick_s)
+
+        def process(unit, t):
+            cols = pl.ds(unit[0] * tb, tb)
+            m_old = m_s[:, cols]
+            m_new = jnp.maximum(m_old, jnp.max(t, axis=0))
+            m_s[:, cols] = m_new
+            m_two = m_new * LOG2E
+            s_s[:, cols] = s_s[:, cols] * jnp.exp2(m_old * LOG2E - m_two) + jnp.sum(jnp.exp2(t * LOG2E - m_two[None]), axis=0)
+
+        pipeline(process)
+
+        @pl.when(j == n_tiles - 1)
+        def _():
+            top = jnp.max(m_s[...], axis=0, keepdims=True)
+            total = jnp.sum(s_s[...] * jnp.exp2((m_s[...] - top) * LOG2E), axis=0, keepdims=True)
+            lse = top * LOG2E + jnp.log2(total)
+            bias_s[0:1, :] = lse - jnp.log2(coef_ref[...])
+            bias_s[1:2, :] = lse
+            dhn_ref[...] = jnp.zeros_like(dhn_ref)
+
+    @pl.when(phase == 1)
+    def _():
+        def back(b):
+            cols = pl.ds(b * tb, tb)
+            dhn_ref[cols, :] += lax.dot_general(dl_ref[:, cols], e_ref[...], TOK_CONTRACT, preferred_element_type=jnp.float32)
+
+        sub = lax.broadcasted_iota(jnp.int32, (8, tb), 0)
+
+        def process(unit, t):
+            b, r = unit
+            cols = pl.ds(b * tb, tb)
+            if r == 0 and b > 0:
+                back(b - 1)
+            rel = lab_ref[:, cols] - (j * vt + r * ur) - sub
+            row = lax.broadcasted_iota(jnp.int32, (ur // 8, 8, tb), 0) * 8
+            is_label = row == rel[None]
+            prob = jnp.exp2(t * LOG2E - bias_s[0:1, cols][None])
+            dl = jnp.where(is_label, prob - coef_ref[:, cols][None], prob)
+            pick = pick_s[:, cols]
+            for g in range(ur // 8):
+                pick = jnp.where(is_label[g], t[g], pick)
+            pick_s[:, cols] = pick
+            dl_ref[r * ur : (r + 1) * ur, cols] = dl.reshape(ur, tb).astype(jnp.bfloat16)
+
+        pipeline(process)
+        back(n_tok // tb - 1)
+
+        @pl.when(j == n_tiles - 1)
+        def _():
+            picked = jnp.sum(pick_s[...], axis=0, keepdims=True)
+            loss_ref[...] = coef_ref[...] * (bias_s[1:2, :] * LN2 - picked)
+
+
+def head(h_norm_t, table, tok_labels, tok_coef):
+    n_tok, vocab = h_norm_t.shape[1], table.shape[0]
+    whole = lambda p, j: (0, 0)
+    return pl.pallas_call(
+        head_kernel,
+        grid=(2, vocab // VOCAB_TILE),
+        in_specs=[pl.BlockSpec((256, n_tok), whole), pl.BlockSpec((VOCAB_TILE, 256), lambda p, j: (j, 0)), pl.BlockSpec((1, n_tok), whole), pl.BlockSpec((1, n_tok), whole)],
+        out_specs=[pl.BlockSpec((VOCAB_TILE, n_tok), lambda p, j: (p * j, 0)), pl.BlockSpec((n_tok, 256), whole), pl.BlockSpec((1, n_tok), whole)],
+        out_shape=(jax.ShapeDtypeStruct((vocab, n_tok), jnp.bfloat16), jax.ShapeDtypeStruct((n_tok, 256), jnp.float32), jax.ShapeDtypeStruct((1, n_tok), jnp.float32)),
+        scratch_shapes=[pltpu.VMEM((8, n_tok), jnp.float32)] * 3 + [pltpu.VMEM((2, n_tok), jnp.float32)],
+        compiler_params=pltpu.CompilerParams(dimension_semantics=("arbitrary", "arbitrary"), vmem_limit_bytes=60 * 1024 * 1024),
+        name="head",
+    )(h_norm_t, table, tok_labels, tok_coef)
 
 
 def mlp_backward(saved, d_hidden, gain_mlp, w_gate, w_up, w_down):
@@ -374,6 +507,12 @@
     return grad_x, grad_gate, grad_up, grad_down
 
 
+def three_parts(wide):
+    high = lax.reduce_precision(wide, 8, 7)
+    middle = lax.reduce_precision(wide - high, 8, 7)
+    return jnp.concatenate([high, middle, wide - high - middle], axis=1).astype(jnp.bfloat16)
+
+
 def rows_to_tiles(rows):
     return rows.reshape(-1, 8, 8, 256).transpose(0, 2, 1, 3).reshape(-1, 64, 256)
 
@@ -394,16 +533,12 @@
         down_full = w_blocks[:, 128:192].reshape(-1, 256)
         emb_rows = jnp.take(table_full, tok_ids, axis=0)
         saved, h_norm = mlp_forward(emb_rows, gain_mlp, gain_head, gate_full, up_full, down_full)
-        loss_part, d_logits = head_forward(h_norm, table_full, tok_labels, tok_coef)
-        d_hnorm = jnp.dot(d_logits, table_full, preferred_element_type=jnp.float32)
-        head_grad = lax.dot_general(d_logits, h_norm, TOK_CONTRACT, preferred_element_type=jnp.float32)
+        d_logits_t, d_hnorm, tok_loss = head(h_norm.T, table_full, tok_labels[None], tok_coef[None])
         d_hidden = rms_back(saved[7], saved[8], gain_head, d_hnorm)
         grad_x, grad_gate, grad_up, grad_down = mlp_backward(saved, d_hidden, gain_mlp, gate_full, up_full, down_full)
-        grad_table = head_grad + jax.ops.segment_sum(grad_x, tok_ids, num_segments=table_full.shape[0])
-        grad_w = jnp.concatenate([rows_to_tiles(grad_gate), rows_to_tiles(grad_up), grad_down.reshape(-1, 64, 256)], axis=1)
-        out, loss = scatter_all(grad_table.reshape(4, 2, 2, 2, E_ROWS, 256), grad_w.reshape(4, 2, 2, 2, W_ROWS, 256), jnp.broadcast_to(loss_part, (8, 128)))
-        g_tab = out[:E_CHUNKS].reshape(E_ROWS, 256)
-        return loss[0, 0], g_tab, tiles_to_rows(out[E_CHUNKS]), tiles_to_rows(out[E_CHUNKS + 1]), out[E_CHUNKS + 2]
+        out, loss = scatter_all(d_logits_t, h_norm, three_parts(0.5 * grad_x), tok_ids[None], rows_to_tiles(grad_gate), rows_to_tiles(grad_up), grad_down, jnp.broadcast_to(jnp.sum(tok_loss), (8, 128)))
+        g_tab = out[W_CHUNKS:].reshape(E_ROWS, 256)
+        return loss[0, 0], g_tab, tiles_to_rows(out[0]), tiles_to_rows(out[1]), out[2]
 
     row_spec = P("fsdp", None)
     tok_spec = P("fsdp")

time: 441 us -> 330 us (0.75)
  other arithmetic: 106 us -> 11.4 us
  matrix products: 105 us -> 26.9 us
  Pallas kernels: 207 us -> 270 us
    dot_general x3 -> x0, matrix products: 82.3 us -> none  [the longest x1 36.6 us: head_forward(): lax.dot_general(h_norm, emb_table, ROW_CONTRACT, preferred_element_type=j...]
    pallas_call x0 -> x1, Pallas kernels: none -> 62.1 us  [head(): pl.pallas_call(head_kernel, grid=(2, vocab // VOCAB_TILE), in_specs=[pl.B...]
    convert_element_type x2, other arithmetic: 42.5 us -> 1.2 us  [rms_scale(): return ((rows_wide * inv_rms * norm_gain).astype(jnp.bfloat16), inv_rms)]
    reduce_sum x2, other arithmetic: 32.8 us -> 2.22 us  [the longest x1 1.61 us: rms_back(): jnp.mean(scaled_grad * rows_wide, axis=-1, keepdims=True)]
    scatter-add x1 -> x0, other arithmetic: 20.1 us -> none  [device_step(): jax.ops.segment_sum(grad_x, tok_ids, num_segments=table_full.shape[0])]
    gather x2 -> x1, local copies, waits for them, and re-layouts: 8.99 us -> 8.78 us  [device_step(): emb_rows = jnp.take(table_full, tok_ids, axis=0)]
where the time goes in v2:
time: 330 us
  Pallas kernels  270 us (82%)
  matrix products  26.9 us (8%)
  local copies, waits for them, and re-layouts  21.1 us (6%)
  other arithmetic  11.4 us (3%)
    pallas_call x1, Pallas kernels, scatter_all(): pl.pallas_call(scatter_kernel, out_shape=(jax.ShapeDtypeStruct((N_CHUNKS,...  134 us
    pallas_call x1, Pallas kernels, gather_all(): pl.pallas_call(gather_kernel, out_shape=(jax.ShapeDtypeStruct((N_DEV, E_R...  73.4 us
    pallas_call x1, Pallas kernels, head(): pl.pallas_call(head_kernel, grid=(2, vocab // VOCAB_TILE), in_specs=[pl.B...  62.1 us
    gather x1, local copies, waits for them, and re-layouts, device_step(): emb_rows = jnp.take(table_full, tok_ids, axis=0)  8.78 us

profile of v2, /device:TPU:0, one launch (start us, length us, event | category | flops | bytes accessed | tf_op | source)
XLA Modules:
  0.0 329.9 jit_solution(3177847040419224752)
XLA Ops:
  0.6 0.0 copy-start.7
  0.6 1.4 pad_maximum_fusion.1.w_ref
  2.1 1.3 convert_reduce_fusion
  3.4 1.2 broadcast_in_dim.36.m_ref
  4.6 73.4 %gather_all.1 = (bf16[32,640,256]{2,1,0:T(8,128)(2,1)}, bf16[32,192,256]{2,1,0:T(8,128)(2,1)}, f32[8,128]{1,0:T(8,128)}) custom-call(bf16[640,256]{1,0:T(8,128)(2,1)} %e_ref.1, bf16[192,256]{1,0:T(8,128)(2,1)} %pad_maximum_fusion.1.w_ref, f32[8,128]{1,0:T(8,128)} %broadcast_in_dim.36.m_ref), custom_call_target="tpu_custom_call" | custom-call | tf_op jit(solution)/shard_map/gather_all/pallas_call | solution.py:151
  78.0 0.7 fusion.33
  78.7 8.8 %gather_fusion = bf16[1024,256]{1,0:T(8,128)(2,1)S(1)} fusion(bf16[20480,256]{1,0:T(8,128)(2,1)} %bitcast.67, s32[1024]{0:T(1024)S(1)} %fusion.33), kind=kCustom, calls=%fused_computation | custom fusion | bytes 1052672 | tf_op jit(solution)/shard_map/jit(_take)/gather | solution.py:534
  87.5 0.0 copy-done.7
  87.5 0.0 copy-start.10
  87.6 0.4 fusion.20
  87.9 2.1 fusion.45
  90.1 0.0 copy-start.3
  90.1 0.0 copy-start.5
  90.1 0.0 copy-done.10
  90.1 1.3 convolution_convert_fusion.1
  91.4 0.0 copy-start
  91.4 0.0 copy-done.3
  91.4 4.8 %fusion = (bf16[1024,2048]{1,0:T(8,128)(2,1)S(1)}, bf16[1024,2048]{1,0:T(8,128)(2,1)}) fusion(bf16[1024,2048]{1,0:T(8,128)(2,1)S(1)} %convolution_convert_fusion.1, bf16[256,2048]{1,0:T(8,128)(2,1)S(1)} %bitcast.74, f32[256]{0:T(256)S(1)} %copy-done.10, f32[1024]{0:T(1024)S(1)} %get-tuple-element.34, bf16[1024,256]{1,0:T(8,128)(2,1)S(1)} %gather_fusion, ...), kind=kOutput, calls=%fused_computation.7 | convolution fusion | flops 1093926912 | bytes 14161920 | tf_op jit(solution)/shard_map/dot_general | solution.py:394
  96.2 0.0 copy-done
  96.2 0.0 copy-start.12
  96.2 0.0 copy-done.5
  96.2 0.0 copy-start.9
  96.2 0.0 copy-start.8
  96.2 1.3 fusion.15
  97.6 0.7 copy-done.12
  98.3 0.0 copy-done.9
  98.3 0.2 fusion.59
  98.5 1.0 copy.15.ht_ref
  99.5 1.2 slice.30
  100.7 0.0 copy-done.8
  100.7 1.2 convert_divide_fusion
  102.0 62.1 %head.1 = (bf16[20480,1024]{1,0:T(8,128)(2,1)}, f32[1024,256]{1,0:T(8,128)}, f32[1,1024]{1,0:T(1,128)}) custom-call(bf16[256,1024]{1,0:T(8,128)(2,1)} %copy.15.ht_ref, bf16[20480,256]{1,0:T(8,128)(2,1)} %bitcast.68, s32[1,1024]{1,0:T(1,128)} %bitcast.85, f32[1,1024]{1,0:T(1,128)} %bitcast.84), custom_call_target="tpu_custom_call" | custom-call | tf_op jit(solution)/shard_map/head/pallas_call | solution.py:484
  164.1 0.0 copy-start.13
  164.1 1.6 fusion.16
  165.7 0.0 copy-start.1
  165.7 0.0 copy-start.2
  165.7 0.0 copy-start.6
  165.7 5.8 %fusion.29 = f32[2048,256]{1,0:T(8,128)} fusion(bf16[1024,2048]{1,0:T(8,128)(2,1)} %copy-done.12, bf16[1024,256]{1,0:T(8,128)(2,1)S(1)} %get-tuple-element.40, f32[1024,256]{1,0:T(8,128)} %get-tuple-element.17, f32[256]{0:T(256)S(1)} %copy-done.9, f32[1024]{0:T(1024)S(1)} %get-tuple-element.36, f32[1024]{0:T(1024)S(1)} %broadcast_multiply_fusion.1, ...), kind=kOutput, calls=%fused_computation.54 | convolution fusion | flops 1075576832 | bytes 7877632 | tf_op jit(solution)/shard_map/dot_general | solution.py:500
  171.6 0.0 copy-done.13
  171.6 0.0 copy-done.1
  171.6 0.0 copy-done.2
  171.6 0.0 copy-done.6
  171.6 5.4 %fusion.9 = (bf16[1024,2048]{1,0:T(8,128)(2,1)S(1)}, bf16[1024,2048]{1,0:T(8,128)(2,1)S(1)}) fusion(bf16[1024,2048]{1,0:T(8,128)(2,1)S(1)} %copy-done.1, bf16[1024,2048]{1,0:T(8,128)(2,1)S(1)} %copy-done.13, bf16[2048,256]{1,0:T(8,128)(2,1)S(1)} %bitcast.77, f32[1024]{0:T(1024)S(1)} %broadcast_multiply_fusion.1, f32[1024]{0:T(1024)S(1)} %get-tuple-element.35, ...), kind=kOutput, calls=%fused_computation.16 | convolution fusion | flops 1107034112 | bytes 19411968 | tf_op jit(solution)/shard_map/dot_general | solution.py:499
  177.0 2.8 fusion.36
  179.8 2.8 fusion.38
  182.6 0.0 copy-start.4
  182.6 1.3 fusion.46
  183.9 0.0 copy-done.4
  183.9 1.4 fusion.28
  185.3 0.0 copy-start.11
  185.3 1.4 reduce-precision_convert_fusion.1
  186.7 0.2 reduce-precision_convert_fusion
  186.9 1.2 pad_maximum_fusion.dx_ref
  188.2 0.0 copy-done.11
  188.2 0.6 reduce_sum.59
  188.8 1.2 broadcast_in_dim.42.l_ref
  190.0 1.0 fusion.14.hn_ref
  191.0 134.1 %scatter_all.1 = (f32[13,64,256]{2,1,0:T(8,128)}, f32[8,128]{1,0:T(8,128)}) custom-call(bf16[4,2,2,2,640,1024]{5,4,3,2,1,0:T(8,128)(2,1)} %bitcast.66, bf16[1024,256]{1,0:T(8,128)(2,1)} %fusion.14.hn_ref, bf16[1024,768]{1,0:T(8,128)(2,1)} %pad_maximum_fusion.dx_ref, s32[1,1024]{1,0:T(1,128)} %bitcast.81, f32[4,2,2,2,64,256]{5,4,3,2,1,0:T(8,128)} %bitcast.73, ...), custom_call_target="tpu_custom_call" | custom-call | tf_op jit(solution)/shard_map/scatter_all/pallas_call | solution.py:346
  325.2 2.0 slice.32
  327.1 1.6 slice_bitcast_fusion
  328.7 1.2 slice.31
  (5 shorter events, 0.0 us)
Async XLA Ops:
  0.6 86.9 %copy-start.7 = (s32[1024]{0:T(1024)S(1)}, s32[1024]{0:T(1024)}, u32[]{:S(2)}) copy-start(s32[1024]{0:T(1024)} %param.9) | copy-start | bytes 12292
  87.5 2.6 copy-start.10
  90.1 1.4 copy-start.3
  90.1 6.1 %copy-start.5 = (bf16[32,64,256]{2,1,0:T(8,128)(2,1)}, bf16[32,64,256]{2,1,0:T(8,128)(2,1)S(1)}, u32[]{:S(2)}) copy-start(bf16[32,64,256]{2,1,0:T(8,128)(2,1)S(1)} %get-tuple-element.25) | copy-start | bytes 3145732
  91.4 4.8 %copy-start = (bf16[1024,2048]{1,0:T(8,128)(2,1)}, bf16[1024,2048]{1,0:T(8,128)(2,1)S(1)}, u32[]{:S(2)}) copy-start(bf16[1024,2048]{1,0:T(8,128)(2,1)S(1)} %convolution_convert_fusion.1) | copy-start | bytes 12582916
  96.2 2.1 copy-start.12
  96.2 2.1 copy-start.9
  96.2 4.5 %copy-start.8 = (s32[1024]{0:T(1024)S(1)}, s32[1024]{0:T(1024)}, u32[]{:S(2)}) copy-start(s32[1024]{0:T(1024)} %param.11) | copy-start | bytes 12292
  164.1 7.5 %copy-start.13 = (bf16[1024,2048]{1,0:T(8,128)(2,1)S(1)}, bf16[1024,2048]{1,0:T(8,128)(2,1)}, u32[]{:S(2)}) copy-start(bf16[1024,2048]{1,0:T(8,128)(2,1)} %get-tuple-element.38) | copy-start | bytes 12582916
  165.7 5.9 %copy-start.1 = (bf16[1024,2048]{1,0:T(8,128)(2,1)S(1)}, bf16[1024,2048]{1,0:T(8,128)(2,1)}, u32[]{:S(2)}) copy-start(bf16[1024,2048]{1,0:T(8,128)(2,1)} %copy-done) | copy-start | bytes 12582916
  165.7 5.9 %copy-start.2 = (f32[1024,256]{1,0:T(8,128)S(1)}, f32[1024,256]{1,0:T(8,128)}, u32[]{:S(2)}) copy-start(f32[1024,256]{1,0:T(8,128)} %get-tuple-element.17) | copy-start | bytes 3145732
  165.7 5.9 %copy-start.6 = (bf16[32,64,256]{2,1,0:T(8,128)(2,1)S(1)}, bf16[32,64,256]{2,1,0:T(8,128)(2,1)}, u32[]{:S(2)}) copy-start(bf16[32,64,256]{2,1,0:T(8,128)(2,1)} %copy-done.5) | copy-start | bytes 3145732
  182.6 1.3 copy-start.4
  185.3 2.9 copy-start.11

commit v3 on v2

--- a/solution.py
+++ b/solution.py
@@ -15,20 +15,23 @@
 E_ROWS = 640
 W_ROWS = 192
 SPLIT = 416
-CHUNK = 64
+CHUNK = 32
 HALF = CHUNK // 2
 E_CHUNKS = E_ROWS // CHUNK
 N_CHUNKS = (E_ROWS + W_ROWS) // CHUNK
 LAG = 2
-AHEAD = 2
-W_CHUNKS = 3
+AHEAD = 3
+W_CHUNKS = W_ROWS // CHUNK
+PER_W = 64 // CHUNK
+Z_PART = 128 // CHUNK
 LOG2E = 1.4426950408889634
+RANGE = 40.0
 LN2 = 0.6931471805599453
 VOCAB_TILE = 2048
 UNIT = 512
 TOK_TILE = 256
-PIECES = 4
-ORDER = (3, 0, 1, 2)
+PIECES = 6
+ORDER = (5, 0, 1, 2, 3, 4)
 
 
 def dev_index(z, y, x, c):
@@ -53,22 +56,21 @@
     pl.semaphore_wait(barrier, 6)
 
 
-def gather_kernel(e_ref, w_ref, m_ref, eo_ref, wo_ref, n_ref, tiles, send_sem, recv_sem, own_sem):
+def gather_kernel(e_ref, g_ref, u_ref, d_ref, mask_ref, eo_ref, go_ref, uo_ref, do_ref, n_ref, m_ref, tiles, send_sem, recv_sem, own_sem):
     z, y, x, c = my_coords()
     me = dev_index(z, y, x, c)
     zs = (z,) + z_partners(z)
+    m_ref[...] = jnp.full_like(m_ref, jnp.sum(mask_ref[...].astype(jnp.float32)))
     greet(z, y, x, c)
 
-    own_src = (e_ref.at[pl.ds(0, SPLIT)], e_ref.at[pl.ds(SPLIT, E_ROWS - SPLIT)], w_ref, m_ref)
+    own_src = (e_ref.at[pl.ds(0, SPLIT)], e_ref.at[pl.ds(SPLIT, E_ROWS - SPLIT)], g_ref, u_ref, d_ref, m_ref)
 
     def place(piece, block):
         if piece == 0:
             return eo_ref.at[block, pl.ds(0, SPLIT)]
         if piece == 1:
             return eo_ref.at[block, pl.ds(SPLIT, E_ROWS - SPLIT)]
-        if piece == 2:
-            return wo_ref.at[block]
-        return tiles.at[block]
+        return (go_ref, uo_ref, do_ref, tiles)[piece - 2].at[block]
 
     sent = []
     counts = [0] * PIECES
@@ -87,10 +89,10 @@
     to_core = dev_index(z, y, x, 1 - c)
     to_x = dev_index(z, y, 1 - x, c)
     to_y = dev_index(z, 1 - y, x, c)
-    hops = ((to_y, to_x), (to_x, to_y), (to_x, to_y), (to_y, to_x))
+    hops = ((to_y, to_x), (to_x, to_y), (to_x, to_y), (to_x, to_y), (to_x, to_y), (to_y, to_x))
 
     def block_at(piece, depth, k, j=0):
-        if piece in (0, 3):
+        if piece in (0, 5):
             ys, xs = ((y, x), (1 - y, x), ((y, 1 - y)[j], 1 - x))[depth]
         else:
             ys, xs = ((y, x), (y, 1 - x), (1 - y, (x, 1 - x)[j]))[depth]
@@ -145,15 +147,17 @@
     n_ref[...] = lax.fori_loop(0, N_DEV, total, jnp.zeros_like(n_ref))
 
 
-def gather_all(e_shard, w_shard, mask_tile):
+def gather_all(e_shard, gate_shard, up_shard, down_shard, mask_tile):
     vmem = pl.BlockSpec(memory_space=pltpu.VMEM)
     anyspace = pl.BlockSpec(memory_space=pl.ANY)
+    shards = (e_shard, gate_shard, up_shard, down_shard)
     return pl.pallas_call(
         gather_kernel,
-        out_shape=(jax.ShapeDtypeStruct((N_DEV, E_ROWS, 256), jnp.bfloat16), jax.ShapeDtypeStruct((N_DEV, W_ROWS, 256), jnp.bfloat16), jax.ShapeDtypeStruct((8, 128), jnp.float32)),
-        in_specs=[vmem, vmem, vmem],
-        out_specs=(anyspace, anyspace, vmem),
+        out_shape=(*(jax.ShapeDtypeStruct((N_DEV, *a.shape), a.dtype) for a in shards), jax.ShapeDtypeStruct((8, 128), jnp.float32)),
+        in_specs=[vmem] * 5,
+        out_specs=(*(anyspace for _ in shards), vmem),
         scratch_shapes=[
+            pltpu.VMEM((8, 128), jnp.float32),
             pltpu.VMEM((N_DEV, 8, 128), jnp.float32),
             pltpu.SemaphoreType.DMA((PIECES, N_DEV)),
             pltpu.SemaphoreType.DMA((PIECES, N_DEV)),
@@ -161,10 +165,10 @@
         ],
         compiler_params=pltpu.CompilerParams(collective_id=0, has_side_effects=True),
         name="gather_all",
-    )(e_shard, w_shard, mask_tile)
-
-
-def scatter_kernel(dl_ref, hn_ref, dx_ref, id_ref, gg_ref, gu_ref, gd_ref, l_ref, out_ref, loss_ref, acc, r0, r1a, r1b, r2, r3, bufs, dl_buf, away_buf, hot, own_sem, load_sem, s0, q0, s1, q1, s2, q2, s3, q3, small_send, small_recv):
+    )(*shards, mask_tile)
+
+
+def scatter_kernel(dl_ref, hn_ref, dx_ref, id_ref, gg_ref, gu_ref, gd_ref, l_ref, oe_ref, ow_ref, loss_ref, acc, r0, r1a, r1b, r2, r3, bufs, dl_buf, away_buf, hot, dx_parts, own_sem, load_sem, s0, q0, s1, q1, s2, q2, s3, q3, small_send, small_recv):
     z, y, x, c = my_coords()
     to_core = dev_index(z, y, x, 1 - c)
     to_x = dev_index(z, y, 1 - x, c)
@@ -192,26 +196,26 @@
 
         row = lax.broadcasted_iota(jnp.int32, (CHUNK, id_ref.shape[1]), 0)
         hn = hn_ref[...]
-        dx = dx_ref[...]
+        dx = dx_parts[...]
         for mine in range(2):
             core = c if mine else 1 - c
 
             def part(zp, carry, mine=mine, core=core):
-                for i in range(8):
-                    dev = dev_index(2 * zp + i // 4, (i // 2) % 2, i % 2, core)
+                for i in range(4 * Z_PART):
+                    dev = dev_index(Z_PART * zp + i // 4, (i // 2) % 2, i % 2, core)
                     here = row == id_ref[...] - (dev * E_ROWS + (k - W_CHUNKS) * CHUNK)
                     hot[i * CHUNK : (i + 1) * CHUNK] = jnp.where(here, 1.0, 0.0).astype(jnp.bfloat16)
-                head = jnp.dot(dl_buf[slot, pl.ds(2 * zp, 2), :, :, core].reshape(8 * CHUNK, -1), hn, preferred_element_type=jnp.float32)
+                head = jnp.dot(dl_buf[slot, pl.ds(Z_PART * zp, Z_PART), :, :, core].reshape(512, -1), hn, preferred_element_type=jnp.float32)
                 rows = jnp.dot(hot[...], dx, preferred_element_type=jnp.float32)
                 rows = rows[:, 0:256] + (rows[:, 256:512] + rows[:, 512:768])
-                total = (head + 2.0 * rows).reshape(2, 2, 2, CHUNK, 256)
+                total = (head + 2.0 * rows).reshape(Z_PART, 2, 2, CHUNK, 256)
                 if mine:
-                    acc[k, pl.ds(2 * zp, 2)] = total
+                    acc[k, pl.ds(Z_PART * zp, Z_PART)] = total
                 else:
-                    away_buf[slot, pl.ds(2 * zp, 2)] = total
+                    away_buf[slot, pl.ds(Z_PART * zp, Z_PART)] = total
                 return carry
 
-            lax.fori_loop(0, 2, part, 0)
+            lax.fori_loop(0, 4 // Z_PART, part, 0)
             if not mine:
                 core_away(k, away_buf.at[slot]).start()
 
@@ -246,16 +250,24 @@
     small_steps[0][0].start()
     w_refs = (gg_ref, gu_ref, gd_ref)
     for k in range(W_CHUNKS):
-        core_away(k, w_refs[k].at[:, :, :, 1 - c]).start()
-        pltpu.make_async_copy(w_refs[k].at[:, :, :, c], acc.at[k], own_sem.at[k]).start()
+        rows = pl.ds(k % PER_W * CHUNK, CHUNK)
+        core_away(k, w_refs[k // PER_W].at[:, :, :, 1 - c, rows]).start()
+        pltpu.make_async_copy(w_refs[k // PER_W].at[:, :, :, c, rows], acc.at[k], own_sem.at[k]).start()
     for k in range(W_CHUNKS, W_CHUNKS + 2):
         load(k).start()
 
+    def cut(i, carry):
+        rows = pl.ds(pl.multiple_of(i * 128, 128), 128)
+        wide = 0.5 * dx_ref[rows, :]
+        for j in range(3):
+            part = wide.astype(jnp.bfloat16)
+            dx_parts[rows, j * 256 : (j + 1) * 256] = part
+            wide = wide - part.astype(jnp.float32)
+        return carry
+
+    lax.fori_loop(0, dx_ref.shape[0] // 128, cut, 0)
+
     def step_body(s, carry):
-        @pl.when((s + AHEAD >= W_CHUNKS) & (s + AHEAD < N_CHUNKS))
-        def _():
-            table_rows(s + AHEAD)
-
         @pl.when(s < W_CHUNKS)
         def _():
             pltpu.make_async_copy(acc.at[s], acc.at[s], own_sem.at[s]).wait()
@@ -307,7 +319,18 @@
             k = s - 3 * LAG
             for copy in along_z(k):
                 copy.wait_recv()
-            out_ref[k] = (r2[k, z] + r3[k, 0]) + (r3[k, 1] + r3[k, 2])
+            total = (r2[k, z] + r3[k, 0]) + (r3[k, 1] + r3[k, 2])
+            @pl.when(k < W_CHUNKS)
+            def _():
+                ow_ref[k] = total
+
+            @pl.when(k >= W_CHUNKS)
+            def _():
+                oe_ref[pl.ds(pl.multiple_of((k - W_CHUNKS) * CHUNK, CHUNK), CHUNK)] = total
+
+        @pl.when((s + AHEAD >= W_CHUNKS) & (s + AHEAD < N_CHUNKS))
+        def _():
+            table_rows(s + AHEAD)
 
         for i in range(3):
 
@@ -324,7 +347,7 @@
 
     for copy in small_steps[3]:
         copy.wait()
-    loss_ref[...] = (bufs[8] + bufs[3]) + (bufs[4] + bufs[5])
+    loss_ref[...] = ((bufs[8] + bufs[3]) + (bufs[4] + bufs[5]))[0:1, 0:1]
 
     for k in (*range(W_CHUNKS), N_CHUNKS - 2, N_CHUNKS - 1):
         core_away(k, r0.at[k]).wait_send()
@@ -337,7 +360,7 @@
     lax.fori_loop(0, N_CHUNKS, finish, 0)
 
 
-def scatter_all(d_logits_t, h_norm, dx_parts, tok_ids, grad_gate, grad_up, grad_down, loss_tile):
+def scatter_all(d_logits_t, h_norm, grad_x, tok_ids, grad_gate, grad_up, grad_down, loss_tile):
     vmem = pl.BlockSpec(memory_space=pltpu.VMEM)
     anyspace = pl.BlockSpec(memory_space=pl.ANY)
     dma = pltpu.SemaphoreType.DMA
@@ -345,9 +368,9 @@
     mesh_rows = (4, 2, 2, 2)
     return pl.pallas_call(
         scatter_kernel,
-        out_shape=(jax.ShapeDtypeStruct((N_CHUNKS, CHUNK, 256), jnp.float32), jax.ShapeDtypeStruct((8, 128), jnp.float32)),
+        out_shape=tuple(jax.ShapeDtypeStruct(shape, jnp.float32) for shape in ((E_ROWS, 256), (W_CHUNKS, CHUNK, 256), (1, 1))),
         in_specs=[anyspace, vmem, vmem, vmem, anyspace, anyspace, anyspace, vmem],
-        out_specs=(vmem, vmem),
+        out_specs=(vmem,) * 3,
         scratch_shapes=[
             pltpu.VMEM((N_CHUNKS, 4, 2, 2, CHUNK, 256), jnp.float32),
             pltpu.VMEM((N_CHUNKS, 4, 2, 2, CHUNK, 256), jnp.float32),
@@ -358,7 +381,8 @@
             pltpu.VMEM((9, 8, 128), jnp.float32),
             pltpu.VMEM((2, *mesh_rows, CHUNK, n_tok), jnp.bfloat16),
             pltpu.VMEM((2, 4, 2, 2, CHUNK, 256), jnp.float32),
-            pltpu.VMEM((8 * CHUNK, n_tok), jnp.bfloat16),
+            pltpu.VMEM((512, n_tok), jnp.bfloat16),
+            pltpu.VMEM((n_tok, 768), jnp.bfloat16),
             dma((W_CHUNKS,)),
             dma((2,)),
             dma((N_CHUNKS,)),
@@ -374,7 +398,7 @@
         ],
         compiler_params=pltpu.CompilerParams(collective_id=1, has_side_effects=True, vmem_limit_bytes=63 * 1024 * 1024),
         name="scatter_all",
-    )(d_logits_t.reshape(*mesh_rows, E_ROWS, n_tok), h_norm, dx_parts, tok_ids, *(g.reshape(*mesh_rows, 64, 256) for g in (grad_gate, grad_up, grad_down)), loss_tile)
+    )(d_logits_t.reshape(*mesh_rows, E_ROWS, n_tok), h_norm, grad_x, tok_ids, *(g.reshape(*mesh_rows, 64, 256) for g in (grad_gate, grad_up, grad_down)), loss_tile)
 
 
 def rms_scale(rows_wide, norm_gain):
@@ -399,7 +423,7 @@
     return (emb_wide, inv_first, a_norm, gate_wide, up_wide, gate_sig, act_rows, hid_wide, inv_second), h_norm
 
 
-def head_kernel(ht_ref, e_ref, lab_ref, coef_ref, dl_ref, dhn_ref, loss_ref, m_s, s_s, pick_s, bias_s):
+def head_kernel(hn_ref, e_ref, lab_ref, mask_ref, n_ref, dl_ref, dhn_ref, loss_ref, ht_ref, m_s, s_s, pick_s, bias_s, coef_ref, redo):
     phase, j = pl.program_id(0), pl.program_id(1)
     n_tok = ht_ref.shape[1]
     n_tiles = pl.num_programs(1)
@@ -422,19 +446,46 @@
     def _():
         @pl.when(j == 0)
         def _():
+            ht_ref[...] = hn_ref[...].T
+            coef_ref[...] = mask_ref[...].astype(jnp.float32) / n_ref[0:1, 0:1]
             m_s[...] = jnp.full_like(m_s, -jnp.inf)
             s_s[...] = jnp.zeros_like(s_s)
             pick_s[...] = jnp.zeros_like(pick_s)
-
-        def process(unit, t):
-            cols = pl.ds(unit[0] * tb, tb)
-            m_old = m_s[:, cols]
-            m_new = jnp.maximum(m_old, jnp.max(t, axis=0))
-            m_s[:, cols] = m_new
-            m_two = m_new * LOG2E
-            s_s[:, cols] = s_s[:, cols] * jnp.exp2(m_old * LOG2E - m_two) + jnp.sum(jnp.exp2(t * LOG2E - m_two[None]), axis=0)
-
-        pipeline(process)
+            redo[0] = 1
+
+        @pl.when(j > 0)
+        def _():
+            sums, tops = {}, {}
+
+            def process(unit, t):
+                b = unit[0]
+                point = m_s[:, b * tb : (b + 1) * tb] * LOG2E
+                part = jnp.exp2(t[0] * LOG2E - point)
+                top = t[0]
+                for g in range(1, ur // 8):
+                    part += jnp.exp2(t[g] * LOG2E - point)
+                    top = jnp.maximum(top, t[g])
+                sums[b] = sums[b] + part if b in sums else part
+                tops[b] = jnp.maximum(tops[b], top) if b in tops else top
+
+            pipeline(process)
+            over = jnp.max(jnp.concatenate([tops[b] - m_s[:, b * tb : (b + 1) * tb] for b in tops], axis=1))
+            fits = over <= RANGE
+            redo[0] = jnp.where(fits, 0, 1)
+            for b in sums:
+                s_s[:, b * tb : (b + 1) * tb] += jnp.where(fits, sums[b], 0.0)
+
+        @pl.when(redo[0] == 1)
+        def _():
+            def process(unit, t):
+                cols = pl.ds(unit[0] * tb, tb)
+                m_old = m_s[:, cols]
+                m_new = jnp.maximum(m_old, jnp.max(t, axis=0))
+                m_s[:, cols] = m_new
+                m_two = m_new * LOG2E
+                s_s[:, cols] = s_s[:, cols] * jnp.exp2(m_old * LOG2E - m_two) + jnp.sum(jnp.exp2(t * LOG2E - m_two[None]), axis=0)
+
+            pipeline(process)
 
         @pl.when(j == n_tiles - 1)
         def _():
@@ -475,22 +526,25 @@
         @pl.when(j == n_tiles - 1)
         def _():
             picked = jnp.sum(pick_s[...], axis=0, keepdims=True)
-            loss_ref[...] = coef_ref[...] * (bias_s[1:2, :] * LN2 - picked)
-
-
-def head(h_norm_t, table, tok_labels, tok_coef):
-    n_tok, vocab = h_norm_t.shape[1], table.shape[0]
-    whole = lambda p, j: (0, 0)
+            loss_ref[...] = jnp.full_like(loss_ref, jnp.sum(coef_ref[...] * (bias_s[1:2, :] * LN2 - picked)))
+
+
+def head(h_norm, table, tok_labels, loss_mask, mask_total):
+    n_tok, vocab = h_norm.shape[0], table.shape[0]
+
+    def whole(*shape):
+        return pl.BlockSpec(shape, lambda p, j: (0, 0))
+
     return pl.pallas_call(
         head_kernel,
         grid=(2, vocab // VOCAB_TILE),
-        in_specs=[pl.BlockSpec((256, n_tok), whole), pl.BlockSpec((VOCAB_TILE, 256), lambda p, j: (j, 0)), pl.BlockSpec((1, n_tok), whole), pl.BlockSpec((1, n_tok), whole)],
-        out_specs=[pl.BlockSpec((VOCAB_TILE, n_tok), lambda p, j: (p * j, 0)), pl.BlockSpec((n_tok, 256), whole), pl.BlockSpec((1, n_tok), whole)],
-        out_shape=(jax.ShapeDtypeStruct((vocab, n_tok), jnp.bfloat16), jax.ShapeDtypeStruct((n_tok, 256), jnp.float32), jax.ShapeDtypeStruct((1, n_tok), jnp.float32)),
-        scratch_shapes=[pltpu.VMEM((8, n_tok), jnp.float32)] * 3 + [pltpu.VMEM((2, n_tok), jnp.float32)],
+        in_specs=[whole(n_tok, 256), pl.BlockSpec((VOCAB_TILE, 256), lambda p, j: (j, 0)), whole(1, n_tok), whole(1, n_tok), whole(8, 128)],
+        out_specs=[pl.BlockSpec((VOCAB_TILE, n_tok), lambda p, j: (p * j, 0)), whole(n_tok, 256), whole(8, 128)],
+        out_shape=(jax.ShapeDtypeStruct((vocab, n_tok), jnp.bfloat16), jax.ShapeDtypeStruct((n_tok, 256), jnp.float32), jax.ShapeDtypeStruct((8, 128), jnp.float32)),
+        scratch_shapes=[pltpu.VMEM((256, n_tok), jnp.bfloat16)] + [pltpu.VMEM((8, n_tok), jnp.float32)] * 3 + [pltpu.VMEM((2, n_tok), jnp.float32), pltpu.VMEM((1, n_tok), jnp.float32), pltpu.SMEM((1,), jnp.int32)],
         compiler_params=pltpu.CompilerParams(dimension_semantics=("arbitrary", "arbitrary"), vmem_limit_bytes=60 * 1024 * 1024),
         name="head",
-    )(h_norm_t, table, tok_labels, tok_coef)
+    )(h_norm, table, tok_labels, loss_mask, mask_total)
 
 
 def mlp_backward(saved, d_hidden, gain_mlp, w_gate, w_up, w_down):
@@ -507,38 +561,29 @@
     return grad_x, grad_gate, grad_up, grad_down
 
 
-def three_parts(wide):
-    high = lax.reduce_precision(wide, 8, 7)
-    middle = lax.reduce_precision(wide - high, 8, 7)
-    return jnp.concatenate([high, middle, wide - high - middle], axis=1).astype(jnp.bfloat16)
-
-
 def rows_to_tiles(rows):
     return rows.reshape(-1, 8, 8, 256).transpose(0, 2, 1, 3).reshape(-1, 64, 256)
 
 
 def tiles_to_rows(tiles):
-    return tiles.reshape(-1, 8, 8, 256).transpose(0, 2, 1, 3).reshape(-1, 2048)
+    return tiles.reshape(8, 8, 256).transpose(1, 0, 2).reshape(8, 2048)
 
 
 def solution(mesh):
     def device_step(tok_ids, tok_labels, loss_mask, table_shard, gain_mlp, gain_head, gate_shard, up_shard, down_shard):
-        mask_wide = loss_mask.astype(jnp.float32)
-        w_shard = jnp.concatenate([rows_to_tiles(gate_shard)[0], rows_to_tiles(up_shard)[0], down_shard], axis=0)
-        table_blocks, w_blocks, mask_total = gather_all(table_shard, w_shard, jnp.broadcast_to(jnp.sum(mask_wide), (8, 128)))
-        tok_coef = mask_wide / mask_total[0, 0]
+        table_blocks, gate_blocks, up_blocks, down_blocks, mask_total = gather_all(table_shard, gate_shard, up_shard, down_shard, loss_mask.reshape(8, 128))
         table_full = table_blocks.reshape(-1, 256)
-        gate_full = tiles_to_rows(w_blocks[:, 0:64])
-        up_full = tiles_to_rows(w_blocks[:, 64:128])
-        down_full = w_blocks[:, 128:192].reshape(-1, 256)
+        gate_full = gate_blocks.reshape(-1, 2048)
+        up_full = up_blocks.reshape(-1, 2048)
+        down_full = down_blocks.reshape(-1, 256)
         emb_rows = jnp.take(table_full, tok_ids, axis=0)
         saved, h_norm = mlp_forward(emb_rows, gain_mlp, gain_head, gate_full, up_full, down_full)
-        d_logits_t, d_hnorm, tok_loss = head(h_norm.T, table_full, tok_labels[None], tok_coef[None])
+        d_logits_t, d_hnorm, loss_tile = head(h_norm, table_full, tok_labels[None], loss_mask[None], mask_total)
         d_hidden = rms_back(saved[7], saved[8], gain_head, d_hnorm)
         grad_x, grad_gate, grad_up, grad_down = mlp_backward(saved, d_hidden, gain_mlp, gate_full, up_full, down_full)
-        out, loss = scatter_all(d_logits_t, h_norm, three_parts(0.5 * grad_x), tok_ids[None], rows_to_tiles(grad_gate), rows_to_tiles(grad_up), grad_down, jnp.broadcast_to(jnp.sum(tok_loss), (8, 128)))
-        g_tab = out[W_CHUNKS:].reshape(E_ROWS, 256)
-        return loss[0, 0], g_tab, tiles_to_rows(out[0]), tiles_to_rows(out[1]), out[2]
+        d_table, d_weights, loss = scatter_all(d_logits_t, h_norm, grad_x, tok_ids[None], rows_to_tiles(grad_gate), rows_to_tiles(grad_up), grad_down, loss_tile)
+        d_gate, d_up, d_down = d_weights.reshape(3, 64, 256)
+        return loss.reshape(()), d_table, tiles_to_rows(d_gate), tiles_to_rows(d_up), d_down
 
     row_spec = P("fsdp", None)
     tok_spec = P("fsdp")

time: 330 us -> 314 us (0.952)
  local copies, waits for them, and re-layouts: 21.1 us -> 13.2 us
  Pallas kernels: 270 us -> 264 us
  other arithmetic: 11.4 us -> 6.7 us
    slice x4 -> x0, local copies, waits for them, and re-layouts: 6.48 us -> none  [the longest x1 2.14 us: device_step(): down_full = w_blocks[:, 128:192].reshape(-1, 256)]
    pallas_call x3, Pallas kernels: 270 us -> 264 us  [the longest x1 131 us: scatter_all(): pl.pallas_call(scatter_kernel, out_shape=tuple((jax.ShapeDtypeStruct(shap...]
where the time goes in v3:
time: 314 us
  Pallas kernels  264 us (84%)
  matrix products  27 us (9%)
  local copies, waits for them, and re-layouts  13.2 us (4%)
  other arithmetic  6.7 us (2%)
    pallas_call x1, Pallas kernels, scatter_all(): pl.pallas_call(scatter_kernel, out_shape=tuple((jax.ShapeDtypeStruct(shap...  131 us
    pallas_call x1, Pallas kernels, gather_all(): pl.pallas_call(gather_kernel, out_shape=(*(jax.ShapeDtypeStruct((N_DEV, *...  74.7 us
    pallas_call x1, Pallas kernels, head(): pl.pallas_call(head_kernel, grid=(2, vocab // VOCAB_TILE), in_specs=[whol...  59 us
    gather x1, local copies, waits for them, and re-layouts, device_step(): emb_rows = jnp.take(table_full, tok_ids, axis=0)  8.87 us

profile of v3, /device:TPU:0, one launch (start us, length us, event | category | flops | bytes accessed | tf_op | source)
XLA Modules:
  0.0 313.9 jit_solution(1997588053785331670)
XLA Ops:
  0.6 0.0 copy-start.5
  0.6 0.7 compare_and_fusion
  1.3 0.7 fusion.36
  2.0 74.7 %gather_all.1 = (bf16[32,640,256]{2,1,0:T(8,128)(2,1)}, bf16[32,8,2048]{2,1,0:T(8,128)(2,1)}, bf16[32,8,2048]{2,1,0:T(8,128)(2,1)}, bf16[32,64,256]{2,1,0:T(8,128)(2,1)}, f32[8,128]{1,0:T(8,128)}) custom-call(bf16[640,256]{1,0:T(8,128)(2,1)} %e_ref.1, bf16[8,2048]{1,0:T(8,128)(2,1)} %g_ref.1, bf16[8,2048]{1,0:T(8,128)(2,1)} %u_ref.1, bf16[64,256]{1,0:T(8,128)(2,1)} %d_ref.1, ...), custom_call_target="tpu_custom_call" | custom-call | tf_op jit(solution)/shard_map/gather_all/pallas_call | solution.py:154
  76.7 0.0 copy-start.3
  76.8 8.9 %gather_fusion = bf16[1024,256]{1,0:T(8,128)(2,1)S(1)} fusion(bf16[20480,256]{1,0:T(8,128)(2,1)} %bitcast.53, s32[1024]{0:T(1024)S(1)} %fusion.36), kind=kCustom, calls=%fused_computation | custom fusion | bytes 1052672 | tf_op jit(solution)/shard_map/jit(_take)/gather | solution.py:579
  85.6 0.4 fusion.19
  86.0 0.0 copy-done.5
  86.0 0.0 copy-done.3
  86.0 0.0 copy-start.6
  86.0 1.3 convolution_convert_fusion.1
  87.4 0.0 copy-done.6
  87.4 0.0 copy-start
  87.4 0.0 copy-start.7
  87.4 4.8 %fusion = (bf16[1024,2048]{1,0:T(8,128)(2,1)S(1)}, bf16[1024,2048]{1,0:T(8,128)(2,1)}) fusion(bf16[1024,2048]{1,0:T(8,128)(2,1)S(1)} %convolution_convert_fusion.1, bf16[32,8,2048]{2,1,0:T(8,128)(2,1)S(1)} %copy-done.6, f32[256]{0:T(256)S(1)} %copy-done.5, f32[1024]{0:T(1024)S(1)} %get-tuple-element.33, bf16[1024,256]{1,0:T(8,128)(2,1)S(1)} %gather_fusion, ...), kind=kOutput, calls=%fused_computation.7 | convolution fusion | flops 1093926912 | bytes 14161920 | tf_op jit(solution)/shard_map/dot_general | solution.py:418
  92.2 0.0 copy-done
  92.2 0.0 copy-start.9
  92.2 0.0 copy-done.7
  92.2 0.0 copy-start.4
  92.2 1.3 fusion.12
  93.5 0.8 copy-done.9
  94.3 0.0 copy-done.4
  94.3 1.0 fusion.14.hn_ref
  95.3 59.0 %head.1 = (bf16[20480,1024]{1,0:T(8,128)(2,1)}, f32[1024,256]{1,0:T(8,128)}, f32[8,128]{1,0:T(8,128)}) custom-call(bf16[1024,256]{1,0:T(8,128)(2,1)} %fusion.14.hn_ref, bf16[20480,256]{1,0:T(8,128)(2,1)} %bitcast.54, s32[1,1024]{1,0:T(1,128)} %bitcast.64, s32[1,1024]{1,0:T(1,128)} %bitcast.63, f32[8,128]{1,0:T(8,128)} %get-tuple-element.20.n_ref), custom_call_target="tpu_custom_call" | custom-call | tf_op jit(solution)/shard_map/head/pallas_call | solution.py:538
  154.3 0.0 copy-start.10
  154.3 1.6 fusion.18
  155.9 0.0 copy-start.1
  155.9 0.0 copy-start.2
  156.0 0.0 copy-start.8
  156.0 5.8 %fusion.32 = f32[2048,256]{1,0:T(8,128)} fusion(bf16[1024,2048]{1,0:T(8,128)(2,1)} %copy-done.9, bf16[1024,256]{1,0:T(8,128)(2,1)S(1)} %get-tuple-element.39, f32[1024,256]{1,0:T(8,128)} %get-tuple-element.22, f32[1024]{0:T(1024)S(1)} %broadcast_multiply_fusion.1, f32[1024]{0:T(1024)S(1)} %get-tuple-element.34, f32[256]{0:T(256)S(1)} %copy-done.4, ...), kind=kOutput, calls=%fused_computation.52 | convolution fusion | flops 1075576832 | bytes 7877632 | tf_op jit(solution)/shard_map/dot_general | solution.py:554
  161.8 0.0 copy-done.10
  161.8 0.0 copy-done.1
  161.8 0.0 copy-done.2
  161.8 0.0 copy-done.8
  161.8 5.4 %fusion.9 = (bf16[1024,2048]{1,0:T(8,128)(2,1)S(1)}, bf16[1024,2048]{1,0:T(8,128)(2,1)S(1)}) fusion(bf16[1024,2048]{1,0:T(8,128)(2,1)S(1)} %copy-done.1, bf16[1024,2048]{1,0:T(8,128)(2,1)S(1)} %copy-done.10, bf16[2048,256]{1,0:T(8,128)(2,1)S(1)} %bitcast.66, f32[1024]{0:T(1024)S(1)} %broadcast_multiply_fusion.1, f32[1024]{0:T(1024)S(1)} %get-tuple-element.34, ...), kind=kOutput, calls=%fused_computation.16 | convolution fusion | flops 1107034112 | bytes 19411968 | tf_op jit(solution)/shard_map/dot_general | solution.py:553
  167.2 1.3 fusion.29
  168.5 2.8 fusion.41
  171.3 1.4 fusion.26
  172.7 2.8 fusion.39
  175.5 2.3 fusion.25.dx_ref
  177.9 130.7 %scatter_all.1 = (f32[640,256]{1,0:T(8,128)}, f32[6,32,256]{2,1,0:T(8,128)}, f32[1,1]{1,0:T(1,128)}) custom-call(bf16[4,2,2,2,640,1024]{5,4,3,2,1,0:T(8,128)(2,1)} %bitcast.52, bf16[1024,256]{1,0:T(8,128)(2,1)} %fusion.14.hn_ref, f32[1024,256]{1,0:T(8,128)} %fusion.25.dx_ref, s32[1,1024]{1,0:T(1,128)} %bitcast.61, f32[4,2,2,2,64,256]{5,4,3,2,1,0:T(8,128)} %bitcast.56, ...), custom_call_target="tpu_custom_call" | custom-call | tf_op jit(solution)/shard_map/scatter_all/pallas_call | solution.py:369
  308.5 1.6 fusion.47
  310.8 2.0 copy.23
  (4 shorter events, 0.0 us)
Async XLA Ops:
  0.6 85.4 %copy-start.5 = (f32[256]{0:T(256)S(1)}, f32[256]{0:T(256)}, u32[]{:S(2)}) copy-start(f32[256]{0:T(256)} %param.13) | copy-start | bytes 3076
  76.7 9.3 %copy-start.3 = (bf16[32,8,2048]{2,1,0:T(8,128)(2,1)S(1)}, bf16[32,8,2048]{2,1,0:T(8,128)(2,1)}, u32[]{:S(2)}) copy-start(bf16[32,8,2048]{2,1,0:T(8,128)(2,1)} %get-tuple-element.17) | copy-start | bytes 3145732
  86.0 1.3 copy-start.6
  87.4 4.8 %copy-start = (bf16[1024,2048]{1,0:T(8,128)(2,1)}, bf16[1024,2048]{1,0:T(8,128)(2,1)S(1)}, u32[]{:S(2)}) copy-start(bf16[1024,2048]{1,0:T(8,128)(2,1)S(1)} %convolution_convert_fusion.1) | copy-start | bytes 12582916
  87.4 4.8 %copy-start.7 = (bf16[32,64,256]{2,1,0:T(8,128)(2,1)S(1)}, bf16[32,64,256]{2,1,0:T(8,128)(2,1)}, u32[]{:S(2)}) copy-start(bf16[32,64,256]{2,1,0:T(8,128)(2,1)} %get-tuple-element.19) | copy-start | bytes 3145732
  92.2 2.1 copy-start.9
  92.2 2.1 copy-start.4
  154.3 7.5 %copy-start.10 = (bf16[1024,2048]{1,0:T(8,128)(2,1)S(1)}, bf16[1024,2048]{1,0:T(8,128)(2,1)}, u32[]{:S(2)}) copy-start(bf16[1024,2048]{1,0:T(8,128)(2,1)} %get-tuple-element.37) | copy-start | bytes 12582916
  155.9 5.9 %copy-start.1 = (bf16[1024,2048]{1,0:T(8,128)(2,1)S(1)}, bf16[1024,2048]{1,0:T(8,128)(2,1)}, u32[]{:S(2)}) copy-start(bf16[1024,2048]{1,0:T(8,128)(2,1)} %copy-done) | copy-start | bytes 12582916
  155.9 5.9 %copy-start.2 = (f32[1024,256]{1,0:T(8,128)S(1)}, f32[1024,256]{1,0:T(8,128)}, u32[]{:S(2)}) copy-start(f32[1024,256]{1,0:T(8,128)} %get-tuple-element.22) | copy-start | bytes 3145732
  156.0 5.9 %copy-start.8 = (bf16[32,64,256]{2,1,0:T(8,128)(2,1)S(1)}, bf16[32,64,256]{2,1,0:T(8,128)(2,1)}, u32[]{:S(2)}) copy-start(bf16[32,64,256]{2,1,0:T(8,128)(2,1)} %get-tuple-element.19) | copy-start | bytes 3145732

commit v4 on v3

--- a/solution.py
+++ b/solution.py
@@ -28,6 +28,8 @@
 RANGE = 40.0
 LN2 = 0.6931471805599453
 VOCAB_TILE = 2048
+FF_TILE = 512
+VMEM_LIMIT = 66060288
 UNIT = 512
 TOK_TILE = 256
 PIECES = 6
@@ -396,7 +398,7 @@
             dma((6,)),
             dma((6,)),
         ],
-        compiler_params=pltpu.CompilerParams(collective_id=1, has_side_effects=True, vmem_limit_bytes=63 * 1024 * 1024),
+        compiler_params=pltpu.CompilerParams(collective_id=1, has_side_effects=True, vmem_limit_bytes=VMEM_LIMIT),
         name="scatter_all",
     )(d_logits_t.reshape(*mesh_rows, E_ROWS, n_tok), h_norm, grad_x, tok_ids, *(g.reshape(*mesh_rows, 64, 256) for g in (grad_gate, grad_up, grad_down)), loss_tile)
 
@@ -413,14 +415,14 @@
 
 def mlp_forward(emb_rows, gain_mlp, gain_head, w_gate, w_up, w_down):
     emb_wide = emb_rows.astype(jnp.float32)
-    a_norm, inv_first = rms_scale(emb_wide, gain_mlp)
-    gate_wide = jnp.dot(a_norm, w_gate, preferred_element_type=jnp.float32).astype(jnp.bfloat16).astype(jnp.float32)
-    up_wide = jnp.dot(a_norm, w_up, preferred_element_type=jnp.float32).astype(jnp.bfloat16).astype(jnp.float32)
+    a_norm = rms_scale(emb_wide, gain_mlp)[0]
+    gate = jnp.dot(a_norm, w_gate, preferred_element_type=jnp.float32).astype(jnp.bfloat16)
+    up = jnp.dot(a_norm, w_up, preferred_element_type=jnp.float32).astype(jnp.bfloat16)
+    gate_wide, up_wide = gate.astype(jnp.float32), up.astype(jnp.float32)
     gate_sig = jax.nn.sigmoid(gate_wide)
     act_rows = (gate_wide * gate_sig * up_wide).astype(jnp.bfloat16)
-    hid_wide = (emb_wide + jnp.dot(act_rows, w_down, preferred_element_type=jnp.float32)).astype(jnp.bfloat16).astype(jnp.float32)
-    h_norm, inv_second = rms_scale(hid_wide, gain_head)
-    return (emb_wide, inv_first, a_norm, gate_wide, up_wide, gate_sig, act_rows, hid_wide, inv_second), h_norm
+    hid = (emb_wide + jnp.dot(act_rows, w_down, preferred_element_type=jnp.float32)).astype(jnp.bfloat16)
+    return gate, up, hid, rms_scale(hid.astype(jnp.float32), gain_head)[0]
 
 
 def head_kernel(hn_ref, e_ref, lab_ref, mask_ref, n_ref, dl_ref, dhn_ref, loss_ref, ht_ref, m_s, s_s, pick_s, bias_s, coef_ref, redo):
@@ -542,23 +544,64 @@
         out_specs=[pl.BlockSpec((VOCAB_TILE, n_tok), lambda p, j: (p * j, 0)), whole(n_tok, 256), whole(8, 128)],
         out_shape=(jax.ShapeDtypeStruct((vocab, n_tok), jnp.bfloat16), jax.ShapeDtypeStruct((n_tok, 256), jnp.float32), jax.ShapeDtypeStruct((8, 128), jnp.float32)),
         scratch_shapes=[pltpu.VMEM((256, n_tok), jnp.bfloat16)] + [pltpu.VMEM((8, n_tok), jnp.float32)] * 3 + [pltpu.VMEM((2, n_tok), jnp.float32), pltpu.VMEM((1, n_tok), jnp.float32), pltpu.SMEM((1,), jnp.int32)],
-        compiler_params=pltpu.CompilerParams(dimension_semantics=("arbitrary", "arbitrary"), vmem_limit_bytes=60 * 1024 * 1024),
+        compiler_params=pltpu.CompilerParams(dimension_semantics=("arbitrary", "arbitrary"), vmem_limit_bytes=VMEM_LIMIT),
         name="head",
     )(h_norm, table, tok_labels, loss_mask, mask_total)
 
 
-def mlp_backward(saved, d_hidden, gain_mlp, w_gate, w_up, w_down):
-    emb_wide, inv_first, a_norm, gate_wide, up_wide, gate_sig, act_rows = saved[:7]
-    hid_grad = d_hidden.astype(jnp.bfloat16)
-    d_act = lax.dot_general(hid_grad, w_down, ROW_CONTRACT, preferred_element_type=jnp.float32)
-    grad_down = lax.dot_general(act_rows, hid_grad, TOK_CONTRACT, preferred_element_type=jnp.float32)
-    d_up = (d_act * gate_wide * gate_sig).astype(jnp.bfloat16)
+def mlp_back_kernel(dhn_ref, h_ref, x_ref, g1_ref, g2_ref, p_ref, q_ref, wg_ref, wu_ref, wd_ref, dx_ref, gg_ref, gu_ref, gd_ref, dh_s, dhb_s, a_s, da_s):
+    j = pl.program_id(0)
+
+    @pl.when(j == 0)
+    def _():
+        hid_wide = h_ref[...].astype(jnp.float32)
+        dh = rms_back(hid_wide, rms_scale(hid_wide, g2_ref[...])[1], g2_ref[...], dhn_ref[...])
+        dh_s[...] = dh
+        dhb_s[...] = dh.astype(jnp.bfloat16)
+        a_s[...] = rms_scale(x_ref[...].astype(jnp.float32), g1_ref[...])[0]
+        da_s[...] = jnp.zeros_like(da_s)
+
+    dhb, a_norm = dhb_s[...], a_s[...]
+    gate_wide, up_wide = p_ref[...].astype(jnp.float32), q_ref[...].astype(jnp.float32)
+    gate_sig = jax.nn.sigmoid(gate_wide)
+    silu = gate_wide * gate_sig
+    d_act = lax.dot_general(dhb, wd_ref[...], ROW_CONTRACT, preferred_element_type=jnp.float32)
+    d_up = (d_act * silu).astype(jnp.bfloat16)
     d_gate = (d_act * up_wide * gate_sig * (1.0 + gate_wide * (1.0 - gate_sig))).astype(jnp.bfloat16)
-    grad_gate = lax.dot_general(a_norm, d_gate, TOK_CONTRACT, preferred_element_type=jnp.float32)
-    grad_up = lax.dot_general(a_norm, d_up, TOK_CONTRACT, preferred_element_type=jnp.float32)
-    d_anorm = lax.dot_general(d_gate, w_gate, ROW_CONTRACT, preferred_element_type=jnp.float32) + lax.dot_general(d_up, w_up, ROW_CONTRACT, preferred_element_type=jnp.float32)
-    grad_x = d_hidden + rms_back(emb_wide, inv_first, gain_mlp, d_anorm)
-    return grad_x, grad_gate, grad_up, grad_down
+    gd_ref[...] = lax.dot_general((silu * up_wide).astype(jnp.bfloat16), dhb, TOK_CONTRACT, preferred_element_type=jnp.float32)
+    gg_ref[...] = lax.dot_general(a_norm, d_gate, TOK_CONTRACT, preferred_element_type=jnp.float32)
+    gu_ref[...] = lax.dot_general(a_norm, d_up, TOK_CONTRACT, preferred_element_type=jnp.float32)
+    da_s[...] += lax.dot_general(d_gate, wg_ref[...], ROW_CONTRACT, preferred_element_type=jnp.float32) + lax.dot_general(d_up, wu_ref[...], ROW_CONTRACT, preferred_element_type=jnp.float32)
+
+    @pl.when(j == pl.num_programs(0) - 1)
+    def _():
+        emb_wide = x_ref[...].astype(jnp.float32)
+        dx_ref[...] = dh_s[...] + rms_back(emb_wide, rms_scale(emb_wide, g1_ref[...])[1], g1_ref[...], da_s[...])
+
+
+def mlp_backward(d_hnorm, hid, emb_rows, gain_mlp, gain_head, gate, up, w_gate, w_up, w_down):
+    n_tok, width = emb_rows.shape
+    d_ff = gate.shape[1]
+
+    def whole(*shape):
+        return pl.BlockSpec(shape, lambda j: (0, 0))
+
+    rows = whole(n_tok, width)
+    gain = whole(1, width)
+    tok_block = pl.BlockSpec((n_tok, FF_TILE), lambda j: (0, j))
+    in_block = pl.BlockSpec((width, FF_TILE), lambda j: (0, j))
+    out_block = pl.BlockSpec((FF_TILE, width), lambda j: (j, 0))
+    wide = jnp.float32
+    return pl.pallas_call(
+        mlp_back_kernel,
+        grid=(d_ff // FF_TILE,),
+        in_specs=[rows, rows, rows, gain, gain, tok_block, tok_block, in_block, in_block, out_block],
+        out_specs=[rows, in_block, in_block, out_block],
+        out_shape=tuple(jax.ShapeDtypeStruct(shape, wide) for shape in ((n_tok, width), (width, d_ff), (width, d_ff), (d_ff, width))),
+        scratch_shapes=[pltpu.VMEM((n_tok, width), kind) for kind in (wide, jnp.bfloat16, jnp.bfloat16, wide)],
+        compiler_params=pltpu.CompilerParams(dimension_semantics=("arbitrary",), vmem_limit_bytes=VMEM_LIMIT),
+        name="mlp_back",
+    )(d_hnorm, hid, emb_rows, gain_mlp[None], gain_head[None], gate, up, w_gate, w_up, w_down)
 
 
 def rows_to_tiles(rows):
@@ -577,10 +620,9 @@
         up_full = up_blocks.reshape(-1, 2048)
         down_full = down_blocks.reshape(-1, 256)
         emb_rows = jnp.take(table_full, tok_ids, axis=0)
-        saved, h_norm = mlp_forward(emb_rows, gain_mlp, gain_head, gate_full, up_full, down_full)
+        gate, up, hid, h_norm = mlp_forward(emb_rows, gain_mlp, gain_head, gate_full, up_full, down_full)
         d_logits_t, d_hnorm, loss_tile = head(h_norm, table_full, tok_labels[None], loss_mask[None], mask_total)
-        d_hidden = rms_back(saved[7], saved[8], gain_head, d_hnorm)
-        grad_x, grad_gate, grad_up, grad_down = mlp_backward(saved, d_hidden, gain_mlp, gate_full, up_full, down_full)
+        grad_x, grad_gate, grad_up, grad_down = mlp_backward(d_hnorm, hid, emb_rows, gain_mlp, gain_head, gate, up, gate_full, up_full, down_full)
         d_table, d_weights, loss = scatter_all(d_logits_t, h_norm, grad_x, tok_ids[None], rows_to_tiles(grad_gate), rows_to_tiles(grad_up), grad_down, loss_tile)
         d_gate, d_up, d_down = d_weights.reshape(3, 64, 256)
         return loss.reshape(()), d_table, tiles_to_rows(d_gate), tiles_to_rows(d_up), d_down

time: 314 us -> 306 us (0.975)
  matrix products: 27 us -> 7.06 us
  Pallas kernels: 264 us -> 280 us
  other arithmetic: 6.7 us -> 2.83 us
    dot_general x6 -> x0, matrix products: 19.5 us -> none  [the longest x1 5.83 us: mlp_backward(): lax.dot_general(act_rows, hid_grad, TOK_CONTRACT, preferred_element_type=...]
    pallas_call x0 -> x1, Pallas kernels: none -> 15.1 us  [mlp_backward(): pl.pallas_call(mlp_back_kernel, grid=(d_ff // FF_TILE,), in_specs=[rows,...]
where the time goes in v4:
time: 306 us; the launch traced here: 305 us
  Pallas kernels  280 us (92%)
  local copies, waits for them, and re-layouts  13.3 us (4%)
  matrix products  7.06 us (2%)
    pallas_call x1, Pallas kernels, scatter_all(): pl.pallas_call(scatter_kernel, out_shape=tuple((jax.ShapeDtypeStruct(shap...  131 us
    pallas_call x1, Pallas kernels, gather_all(): pl.pallas_call(gather_kernel, out_shape=(*(jax.ShapeDtypeStruct((N_DEV, *...  74.7 us
    pallas_call x1, Pallas kernels, head(): pl.pallas_call(head_kernel, grid=(2, vocab // VOCAB_TILE), in_specs=[whol...  59 us
    pallas_call x1, Pallas kernels, mlp_backward(): pl.pallas_call(mlp_back_kernel, grid=(d_ff // FF_TILE,), in_specs=[rows,...  15.1 us
    gather x1, local copies, waits for them, and re-layouts, device_step(): emb_rows = jnp.take(table_full, tok_ids, axis=0)  8.88 us

profile of v4, /device:TPU:0, one launch (start us, length us, event | category | flops | bytes accessed | tf_op | source)
XLA Modules:
  0.0 305.3 jit_solution(18358314991929779450)
XLA Ops:
  0.6 0.0 copy-start.6
  0.6 0.7 compare_and_fusion
  1.3 0.7 fusion.20
  2.0 74.7 %gather_all.1 = (bf16[32,640,256]{2,1,0:T(8,128)(2,1)}, bf16[32,8,2048]{2,1,0:T(8,128)(2,1)}, bf16[32,8,2048]{2,1,0:T(8,128)(2,1)}, bf16[32,64,256]{2,1,0:T(8,128)(2,1)}, f32[8,128]{1,0:T(8,128)}) custom-call(bf16[640,256]{1,0:T(8,128)(2,1)} %e_ref.1, bf16[8,2048]{1,0:T(8,128)(2,1)} %g_ref.1, bf16[8,2048]{1,0:T(8,128)(2,1)} %u_ref.1, bf16[64,256]{1,0:T(8,128)(2,1)} %d_ref.1, ...), custom_call_target="tpu_custom_call" | custom-call | tf_op jit(solution)/shard_map/gather_all/pallas_call | solution.py:156
  76.7 0.0 copy-start.3
  76.7 8.9 %gather_fusion = bf16[1024,256]{1,0:T(8,128)(2,1)S(1)} fusion(bf16[20480,256]{1,0:T(8,128)(2,1)} %bitcast.40, s32[1024]{0:T(1024)S(1)} %fusion.20), kind=kCustom, calls=%fused_computation | custom fusion | bytes 1052672 | tf_op jit(solution)/shard_map/jit(_take)/gather | solution.py:622
  85.6 0.4 fusion.15
  86.1 0.0 copy-start.2
  86.1 0.0 copy-start.5
  86.1 2.7 convolution_convert_fusion.q_ref
  88.8 0.0 copy-done.6
  88.9 0.0 copy-done.3
  88.9 0.0 copy-start
  88.9 1.3 convolution_convert_fusion.1.p_ref
  90.2 0.0 copy-done.5
  90.2 0.0 copy-start.1
  90.2 0.0 copy-start.7
  90.2 3.0 fusion.12
  93.2 0.0 copy-done.2
  93.3 0.0 copy-done
  93.3 0.0 copy-done.1
  93.3 0.0 copy-start.4
  93.3 0.8 copy-done.4
  94.1 0.0 copy-done.7
  94.1 1.0 fusion.14.hn_ref
  95.1 59.0 %head.1 = (bf16[20480,1024]{1,0:T(8,128)(2,1)}, f32[1024,256]{1,0:T(8,128)}, f32[8,128]{1,0:T(8,128)}) custom-call(bf16[1024,256]{1,0:T(8,128)(2,1)} %fusion.14.hn_ref, bf16[20480,256]{1,0:T(8,128)(2,1)} %bitcast.41, s32[1,1024]{1,0:T(1,128)} %bitcast.56, s32[1,1024]{1,0:T(1,128)} %bitcast.55, f32[8,128]{1,0:T(8,128)} %get-tuple-element.24.n_ref), custom_call_target="tpu_custom_call" | custom-call | tf_op jit(solution)/shard_map/head/pallas_call | solution.py:540
  154.1 15.1 %mlp_back.1 = (f32[1024,256]{1,0:T(8,128)}, f32[256,2048]{1,0:T(8,128)}, f32[256,2048]{1,0:T(8,128)}, f32[2048,256]{1,0:T(8,128)}) custom-call(f32[1024,256]{1,0:T(8,128)} %get-tuple-element.26.dhn_ref, bf16[1024,256]{1,0:T(8,128)(2,1)} %copy-done.4, bf16[1024,256]{1,0:T(8,128)(2,1)} %copy-done.2, f32[1,256]{1,0:T(1,128)} %bitcast.53, f32[1,256]{1,0:T(1,128)} %bitcast.57, ...), custom_call_target="tpu_custom_call" | custom-call | tf_op jit(solution)/shard_map/mlp_back/pallas_call | solution.py:595
  169.3 130.6 %scatter_all.1 = (f32[640,256]{1,0:T(8,128)}, f32[6,32,256]{2,1,0:T(8,128)}, f32[1,1]{1,0:T(1,128)}) custom-call(bf16[4,2,2,2,640,1024]{5,4,3,2,1,0:T(8,128)(2,1)} %bitcast.39, bf16[1024,256]{1,0:T(8,128)(2,1)} %fusion.14.hn_ref, f32[1024,256]{1,0:T(8,128)} %get-tuple-element.27.dx_ref, s32[1,1024]{1,0:T(1,128)} %bitcast.52, ...), custom_call_target="tpu_custom_call" | custom-call | tf_op jit(solution)/shard_map/scatter_all/pallas_call | solution.py:371
  299.9 1.6 fusion.24
  302.2 2.0 copy.19
  (2 shorter events, 0.0 us)
Async XLA Ops:
  0.6 88.2 %copy-start.6 = (f32[256]{0:T(256)S(1)}, f32[256]{0:T(256)}, u32[]{:S(2)}) copy-start(f32[256]{0:T(256)} %param.13) | copy-start | bytes 3076
  76.7 12.1 %copy-start.3 = (bf16[32,8,2048]{2,1,0:T(8,128)(2,1)S(1)}, bf16[32,8,2048]{2,1,0:T(8,128)(2,1)}, u32[]{:S(2)}) copy-start(bf16[32,8,2048]{2,1,0:T(8,128)(2,1)} %get-tuple-element.21) | copy-start | bytes 3145732
  86.1 7.2 %copy-start.2 = (bf16[1024,256]{1,0:T(8,128)(2,1)}, bf16[1024,256]{1,0:T(8,128)(2,1)S(1)}, u32[]{:S(2)}) copy-start(bf16[1024,256]{1,0:T(8,128)(2,1)S(1)} %get-tuple-element.36.x_ref) | copy-start | bytes 1572868
  86.1 4.1 %copy-start.5 = (bf16[32,64,256]{2,1,0:T(8,128)(2,1)S(1)}, bf16[32,64,256]{2,1,0:T(8,128)(2,1)}, u32[]{:S(2)}) copy-start(bf16[32,64,256]{2,1,0:T(8,128)(2,1)} %get-tuple-element.23) | copy-start | bytes 3145732
  88.9 4.4 %copy-start = (bf16[1024,2048]{1,0:T(8,128)(2,1)}, bf16[1024,2048]{1,0:T(8,128)(2,1)S(1)}, u32[]{:S(2)}) copy-start(bf16[1024,2048]{1,0:T(8,128)(2,1)S(1)} %convolution_convert_fusion.q_ref) | copy-start | bytes 12582916
  90.2 3.1 %copy-start.1 = (bf16[1024,2048]{1,0:T(8,128)(2,1)}, bf16[1024,2048]{1,0:T(8,128)(2,1)S(1)}, u32[]{:S(2)}) copy-start(bf16[1024,2048]{1,0:T(8,128)(2,1)S(1)} %convolution_convert_fusion.1.p_ref) | copy-start | bytes 12582916
  90.2 3.9 %copy-start.7 = (f32[256]{0:T(256)S(1)}, f32[256]{0:T(256)}, u32[]{:S(2)}) copy-start(f32[256]{0:T(256)} %param.14) | copy-start | bytes 3076
  93.3 0.8 copy-start.4

commit v5 on v4

--- a/solution.py
+++ b/solution.py
@@ -32,8 +32,9 @@
 VMEM_LIMIT = 66060288
 UNIT = 512
 TOK_TILE = 256
-PIECES = 6
-ORDER = (5, 0, 1, 2, 3, 4)
+PIECES = 7
+FIRST = SPLIT // 2
+ORDER = (5, 0, 1, 2, 3, 4, 6)
 
 
 def dev_index(z, y, x, c):
@@ -65,11 +66,13 @@
     m_ref[...] = jnp.full_like(m_ref, jnp.sum(mask_ref[...].astype(jnp.float32)))
     greet(z, y, x, c)
 
-    own_src = (e_ref.at[pl.ds(0, SPLIT)], e_ref.at[pl.ds(SPLIT, E_ROWS - SPLIT)], g_ref, u_ref, d_ref, m_ref)
+    own_src = (e_ref.at[pl.ds(0, FIRST)], e_ref.at[pl.ds(SPLIT, E_ROWS - SPLIT)], g_ref, u_ref, d_ref, m_ref, e_ref.at[pl.ds(FIRST, FIRST)])
 
     def place(piece, block):
         if piece == 0:
-            return eo_ref.at[block, pl.ds(0, SPLIT)]
+            return eo_ref.at[block, pl.ds(0, FIRST)]
+        if piece == 6:
+            return eo_ref.at[block, pl.ds(FIRST, FIRST)]
         if piece == 1:
             return eo_ref.at[block, pl.ds(SPLIT, E_ROWS - SPLIT)]
         return (go_ref, uo_ref, do_ref, tiles)[piece - 2].at[block]
@@ -91,10 +94,11 @@
     to_core = dev_index(z, y, x, 1 - c)
     to_x = dev_index(z, y, 1 - x, c)
     to_y = dev_index(z, 1 - y, x, c)
-    hops = ((to_y, to_x), (to_x, to_y), (to_x, to_y), (to_x, to_y), (to_x, to_y), (to_y, to_x))
+    by_y, by_x = (to_y, to_x), (to_x, to_y)
+    hops = (by_y, by_x, by_x, by_x, by_x, by_y, by_y)
 
     def block_at(piece, depth, k, j=0):
-        if piece in (0, 5):
+        if hops[piece] is by_y:
             ys, xs = ((y, x), (1 - y, x), ((y, 1 - y)[j], 1 - x))[depth]
         else:
             ys, xs = ((y, x), (y, 1 - x), (1 - y, (x, 1 - x)[j]))[depth]

time: 306 us -> 304 us (level)
  no operation moved by 1% of the time
where the time goes in v5:
time: 304 us; the launch traced here: 303 us
  Pallas kernels  277 us (91%)
  local copies, waits for them, and re-layouts  13.3 us (4%)
  matrix products  7.06 us (2%)
    pallas_call x1, Pallas kernels, scatter_all(): pl.pallas_call(scatter_kernel, out_shape=tuple((jax.ShapeDtypeStruct(shap...  131 us
    pallas_call x1, Pallas kernels, gather_all(): pl.pallas_call(gather_kernel, out_shape=(*(jax.ShapeDtypeStruct((N_DEV, *...  72.7 us
    pallas_call x1, Pallas kernels, head(): pl.pallas_call(head_kernel, grid=(2, vocab // VOCAB_TILE), in_specs=[whol...  59 us
    pallas_call x1, Pallas kernels, mlp_backward(): pl.pallas_call(mlp_back_kernel, grid=(d_ff // FF_TILE,), in_specs=[rows,...  15.1 us
    gather x1, local copies, waits for them, and re-layouts, device_step(): emb_rows = jnp.take(table_full, tok_ids, axis=0)  8.88 us

profile of v5, /device:TPU:0, one launch (start us, length us, event | category | flops | bytes accessed | tf_op | source)
XLA Modules:
  0.0 303.2 jit_solution(1068540337871436030)
XLA Ops:
  0.6 0.0 copy-start.6
  0.6 0.7 compare_and_fusion
  1.3 0.7 fusion.20
  2.0 72.7 %gather_all.1 = (bf16[32,640,256]{2,1,0:T(8,128)(2,1)}, bf16[32,8,2048]{2,1,0:T(8,128)(2,1)}, bf16[32,8,2048]{2,1,0:T(8,128)(2,1)}, bf16[32,64,256]{2,1,0:T(8,128)(2,1)}, f32[8,128]{1,0:T(8,128)}) custom-call(bf16[640,256]{1,0:T(8,128)(2,1)} %e_ref.1, bf16[8,2048]{1,0:T(8,128)(2,1)} %g_ref.1, bf16[8,2048]{1,0:T(8,128)(2,1)} %u_ref.1, bf16[64,256]{1,0:T(8,128)(2,1)} %d_ref.1, ...), custom_call_target="tpu_custom_call" | custom-call | tf_op jit(solution)/shard_map/gather_all/pallas_call | solution.py:160
  74.8 0.0 copy-start.3
  74.8 8.9 %gather_fusion = bf16[1024,256]{1,0:T(8,128)(2,1)S(1)} fusion(bf16[20480,256]{1,0:T(8,128)(2,1)} %bitcast.40, s32[1024]{0:T(1024)S(1)} %fusion.20), kind=kCustom, calls=%fused_computation | custom fusion | bytes 1052672 | tf_op jit(solution)/shard_map/jit(_take)/gather | solution.py:626
  83.7 0.4 fusion.15
  84.1 0.0 copy-start.2
  84.1 0.0 copy-start.5
  84.1 2.7 convolution_convert_fusion.q_ref
  86.9 0.0 copy-done.6
  86.9 0.0 copy-done.3
  86.9 0.0 copy-start
  86.9 1.3 convolution_convert_fusion.1.p_ref
  88.2 0.0 copy-done.5
  88.2 0.0 copy-start.1
  88.2 0.0 copy-start.7
  88.2 3.0 fusion.12
  91.3 0.0 copy-done.2
  91.3 0.0 copy-done
  91.3 0.0 copy-done.1
  91.3 0.0 copy-start.4
  91.3 0.8 copy-done.4
  92.1 0.0 copy-done.7
  92.1 1.0 fusion.14.hn_ref
  93.1 59.0 %head.1 = (bf16[20480,1024]{1,0:T(8,128)(2,1)}, f32[1024,256]{1,0:T(8,128)}, f32[8,128]{1,0:T(8,128)}) custom-call(bf16[1024,256]{1,0:T(8,128)(2,1)} %fusion.14.hn_ref, bf16[20480,256]{1,0:T(8,128)(2,1)} %bitcast.41, s32[1,1024]{1,0:T(1,128)} %bitcast.56, s32[1,1024]{1,0:T(1,128)} %bitcast.55, f32[8,128]{1,0:T(8,128)} %get-tuple-element.24.n_ref), custom_call_target="tpu_custom_call" | custom-call | tf_op jit(solution)/shard_map/head/pallas_call | solution.py:544
  152.2 15.1 %mlp_back.1 = (f32[1024,256]{1,0:T(8,128)}, f32[256,2048]{1,0:T(8,128)}, f32[256,2048]{1,0:T(8,128)}, f32[2048,256]{1,0:T(8,128)}) custom-call(f32[1024,256]{1,0:T(8,128)} %get-tuple-element.26.dhn_ref, bf16[1024,256]{1,0:T(8,128)(2,1)} %copy-done.4, bf16[1024,256]{1,0:T(8,128)(2,1)} %copy-done.2, f32[1,256]{1,0:T(1,128)} %bitcast.53, f32[1,256]{1,0:T(1,128)} %bitcast.57, ...), custom_call_target="tpu_custom_call" | custom-call | tf_op jit(solution)/shard_map/mlp_back/pallas_call | solution.py:599
  167.3 130.6 %scatter_all.1 = (f32[640,256]{1,0:T(8,128)}, f32[6,32,256]{2,1,0:T(8,128)}, f32[1,1]{1,0:T(1,128)}) custom-call(bf16[4,2,2,2,640,1024]{5,4,3,2,1,0:T(8,128)(2,1)} %bitcast.39, bf16[1024,256]{1,0:T(8,128)(2,1)} %fusion.14.hn_ref, f32[1024,256]{1,0:T(8,128)} %get-tuple-element.27.dx_ref, s32[1,1024]{1,0:T(1,128)} %bitcast.52, ...), custom_call_target="tpu_custom_call" | custom-call | tf_op jit(solution)/shard_map/scatter_all/pallas_call | solution.py:375
  297.9 1.6 fusion.24
  300.1 2.0 copy.19
  (2 shorter events, 0.0 us)
Async XLA Ops:
  0.6 86.3 %copy-start.6 = (f32[256]{0:T(256)S(1)}, f32[256]{0:T(256)}, u32[]{:S(2)}) copy-start(f32[256]{0:T(256)} %param.13) | copy-start | bytes 3076
  74.8 12.1 %copy-start.3 = (bf16[32,8,2048]{2,1,0:T(8,128)(2,1)S(1)}, bf16[32,8,2048]{2,1,0:T(8,128)(2,1)}, u32[]{:S(2)}) copy-start(bf16[32,8,2048]{2,1,0:T(8,128)(2,1)} %get-tuple-element.21) | copy-start | bytes 3145732
  84.1 7.2 %copy-start.2 = (bf16[1024,256]{1,0:T(8,128)(2,1)}, bf16[1024,256]{1,0:T(8,128)(2,1)S(1)}, u32[]{:S(2)}) copy-start(bf16[1024,256]{1,0:T(8,128)(2,1)S(1)} %get-tuple-element.36.x_ref) | copy-start | bytes 1572868
  84.1 4.1 %copy-start.5 = (bf16[32,64,256]{2,1,0:T(8,128)(2,1)S(1)}, bf16[32,64,256]{2,1,0:T(8,128)(2,1)}, u32[]{:S(2)}) copy-start(bf16[32,64,256]{2,1,0:T(8,128)(2,1)} %get-tuple-element.23) | copy-start | bytes 3145732
  86.9 4.4 %copy-start = (bf16[1024,2048]{1,0:T(8,128)(2,1)}, bf16[1024,2048]{1,0:T(8,128)(2,1)S(1)}, u32[]{:S(2)}) copy-start(bf16[1024,2048]{1,0:T(8,128)(2,1)S(1)} %convolution_convert_fusion.q_ref) | copy-start | bytes 12582916
  88.2 3.1 %copy-start.1 = (bf16[1024,2048]{1,0:T(8,128)(2,1)}, bf16[1024,2048]{1,0:T(8,128)(2,1)S(1)}, u32[]{:S(2)}) copy-start(bf16[1024,2048]{1,0:T(8,128)(2,1)S(1)} %convolution_convert_fusion.1.p_ref) | copy-start | bytes 12582916
  88.2 3.9 %copy-start.7 = (f32[256]{0:T(256)S(1)}, f32[256]{0:T(256)}, u32[]{:S(2)}) copy-start(f32[256]{0:T(256)} %param.14) | copy-start | bytes 3076
  91.3 0.8 copy-start.4
